TPU v7x, 32 devices: a whole 2x2x4 slice. The times are simulated.
32 devices in a mesh: dp: 4 (over y, core), row: 2 (over x), col: 4 (over z).
Axes of the slice: x: 2, y: 2, z: 4, core: 2. Of those that a mesh axis runs over, the one named last changes fastest.
Arguments:
- images: bfloat16 [4, 64, 32, 1024], P('dp', None, 'row', 'col'), may hold values from -6 to 6
- first_kernel: bfloat16 [64, 64, 3, 3], replicated, may hold values from -0.25 to 0.25
- second_kernel: bfloat16 [64, 64, 3, 3], replicated, may hold values from -0.25 to 0.25
- cotangent: bfloat16 [4, 64, 32, 1024], P('dp', None, 'row', 'col'), may hold values from -6 to 6
Outputs:
- outputs: bfloat16 [4, 64, 32, 1024], P('dp', None, 'row', 'col')
- input_grad: bfloat16 [4, 64, 32, 1024], P('dp', None, 'row', 'col')
- first_grad: float32 [64, 64, 3, 3], replicated
- second_grad: float32 [64, 64, 3, 3], replicated
All inputs are finite; a program needn't handle non-finite values.
Results may differ from a plain program's by a relative error of at most 0.005.
Values may be sent and summed in bfloat16 or wider, within the bound.
No kernel may reach another device: no remote copies, remote signals or barrier semaphores. Data moves between devices by JAX's collectives and lax.ppermute only.
A program may use at most 64 MiB of HBM per device.

v0:
```python
import math

import jax
import jax.numpy as jnp
from jax import lax
from jax.sharding import PartitionSpec as P


def extended(array, sides, width):
    for axis, dim in sides:
        size, length = (lax.axis_size(axis), array.shape[dim])
        up = [(i, (i + 1) % size) for i in range(size - 1)]
        down = [(j, i) for i, j in up]
        last = lax.slice_in_dim(array, length - width, length, axis=dim)
        leading = lax.slice_in_dim(array, 0, width, axis=dim)
        before = lax.ppermute(last, axis, up)
        after = lax.ppermute(leading, axis, down)
        array = jnp.concatenate([before, array, after], axis=dim)
    return array


def convolve(padded, kernel):
    return lax.conv_general_dilated(
        padded,
        kernel,
        (1, 1),
        "VALID",
        dimension_numbers=("NCHW", "OIHW", "NCHW"),
        preferred_element_type=jnp.float32,
    )


def flipped(kernel):
    return jnp.flip(kernel, (2, 3)).transpose(1, 0, 2, 3)


def silu_grad(value):
    sigma = jax.nn.sigmoid(value)
    return sigma * (1.0 + value * (1.0 - sigma))


def kernel_grad(padded, upstream):
    height = upstream.shape[2]
    breadth = upstream.shape[3]
    outer = []
    for offset_row in range(3):
        inner = []
        for offset_col in range(3):
            window = padded[
                :, :, offset_row : offset_row + height, offset_col : offset_col + breadth
            ]
            inner.append(
                jnp.einsum("nihw,nohw->oi", window, upstream, preferred_element_type=jnp.float32)
            )
        outer.append(jnp.stack(inner, -1))
    return jnp.stack(outer, 2)


def grid_mask(height, breadth):
    row_index = lax.axis_index("row") * height + jnp.arange(height + 2, dtype=jnp.int32) - 1
    col_index = lax.axis_index("col") * breadth + jnp.arange(breadth + 2, dtype=jnp.int32) - 1
    row_valid = (row_index >= 0) & (row_index < height * lax.axis_size("row"))
    col_valid = (col_index >= 0) & (col_index < breadth * lax.axis_size("col"))
    return (row_valid[:, None] & col_valid[None, :]).astype(jnp.float32)


def on_device(images, first_kernel, second_kernel, cotangent):
    channels = images.shape[1]
    height = images.shape[2]
    breadth = images.shape[3]
    total_pixels = (
        images.shape[0]
        * height
        * breadth
        * lax.axis_size("dp")
        * lax.axis_size("row")
        * lax.axis_size("col")
    )
    factor = 1.0 / math.sqrt(total_pixels)
    stacked = jnp.concatenate((images, cotangent), axis=1)
    both = extended(stacked, (("row", 2), ("col", 3)), 2)
    widened = both[:, :channels]
    widened_cot = both[:, channels:]
    inside = grid_mask(height, breadth)
    hidden = convolve(widened, first_kernel)
    act_padded = (jax.nn.silu(hidden) * inside).astype(jnp.bfloat16)
    padded_in = widened[:, :, 1:-1, 1:-1]
    outputs = convolve(act_padded, second_kernel).astype(jnp.bfloat16)
    second_grad = kernel_grad(act_padded, cotangent)
    act_grad = convolve(widened_cot, flipped(second_kernel))
    hid_padded = (act_grad * silu_grad(hidden) * inside).astype(jnp.bfloat16)
    hid_grad = hid_padded[:, :, 1:-1, 1:-1]
    input_grad = convolve(hid_padded, flipped(first_kernel)).astype(jnp.bfloat16)
    first_grad = kernel_grad(padded_in, hid_grad)
    first_grad, second_grad = lax.psum((first_grad, second_grad), ("dp", "row", "col"))
    return (outputs, input_grad, first_grad * factor, second_grad * factor)


def solution(mesh):
    in_specs = (P("dp", None, "row", "col"), P(), P(), P("dp", None, "row", "col"))
    out_specs = (P("dp", None, "row", "col"), P("dp", None, "row", "col"), P(), P())
    return jax.shard_map(
        on_device, mesh=mesh, in_specs=in_specs, out_specs=out_specs, check_vma=False
    )
```

profile of v0, /device:TPU:0, one launch (start us, length us, event | category | flops | bytes accessed | tf_op | source)
XLA Modules:
  0.0 264.4 jit_solution(4958273212836746187)
XLA Ops:
  7.2 1.2 copy_dynamic-update-slice_fusion.1
  8.5 1.2 copy_dynamic-update-slice_fusion
  9.7 4.9 %collective-permute-start = (bf16[1,128,2,256]{3,1,2,0:T(8,128)(2,1)S(1)}, bf16[1,128,2,256]{3,1,2,0:T(8,128)(2,1)S(1)}, u32[]{:S(2)}, u32[]{:S(2)}) collective-permute-start(bf16[1,128,2,256]{3,1,2,0:T(8,128)(2,1)S(1)} %get-tuple-element.22), channel_id=1, source_target_pairs={{0,4},{1,5},{2,6},{3,7},{8,12},{9,13},{10,14},{11,15},{16,20},{17,... | collective-permute-start | bytes 393224 | tf_op jit(solution)/shard_map/ppermute | solution.py:16
  14.6 1.3 collective-permute-start.1
  15.9 1.4 collective-permute-done
  17.3 4.1 %collective-permute-done.1 = bf16[1,128,2,256]{3,1,2,0:T(8,128)(2,1)S(1)} collective-permute-done((bf16[1,128,2,256]{3,1,2,0:T(8,128)(2,1)S(1)}, bf16[1,128,2,256]{3,1,2,0:T(8,128)(2,1)S(1)}, u32[]{:S(2)}, u32[]{:S(2)}) %collective-permute-start.1) | collective-permute-done | bytes 131104 | tf_op jit(solution)/shard_map/ppermute | solution.py:17
  21.6 0.3 fusion.118
  22.0 0.3 copy.72
  22.2 3.5 %collective-permute-start.2 = (bf16[1,128,20,2]{1,3,2,0:T(2,128)(2,1)S(1)}, bf16[1,128,20,2]{1,3,2,0:T(2,128)(2,1)S(1)}, u32[]{:S(2)}, u32[]{:S(2)}) collective-permute-start(bf16[1,128,20,2]{1,3,2,0:T(2,128)(2,1)S(1)} %copy.72), channel_id=1, source_target_pairs={{0,1},{1,2},{2,3},{4,5},{5,6},{6,7},{8,9},{9,10},{10,11},{12,13},{... | collective-permute-start | bytes 30728 | tf_op jit(solution)/shard_map/ppermute | solution.py:16
  26.0 1.3 collective-permute-start.3
  27.4 0.4 copy.74
  27.8 3.8 %collective-permute-done.3 = bf16[1,128,20,2]{1,3,2,0:T(2,128)(2,1)S(1)} collective-permute-done((bf16[1,128,20,2]{1,3,2,0:T(2,128)(2,1)S(1)}, bf16[1,128,20,2]{1,3,2,0:T(2,128)(2,1)S(1)}, u32[]{:S(2)}, u32[]{:S(2)}) %collective-permute-start.3) | collective-permute-done | bytes 10272 | tf_op jit(solution)/shard_map/ppermute | solution.py:17
  31.6 0.4 copy.75
  32.0 0.9 copy-done.5
  32.9 1.2 pad_maximum_fusion
  34.4 3.5 %reshape.214 = bf16[64,20,1,8,33]{4,3,0,1,2:T(8,128)(2,1)} reshape(bf16[64,20,1,264]{3,0,1,2:T(8,128)(2,1)S(1)} %pad) | data formatting | bytes 1351680 | tf_op jit(solution)/shard_map/conv_general_dilated | solution.py:23
  37.9 4.6 %copy.78 = bf16[64,20,1,8,33]{0,3,4,1,2:T(8,128)(2,1)} copy(bf16[64,20,1,8,33]{4,3,0,1,2:T(8,128)(2,1)} %reshape.214) | data formatting | bytes 1351680 | tf_op jit(solution)/shard_map/conv_general_dilated | solution.py:23
  42.5 0.9 slice.133
  43.6 3.3 %reshape.216 = bf16[64,20,1,8,33]{4,3,0,1,2:T(8,128)(2,1)} reshape(bf16[64,20,1,264]{3,0,1,2:T(8,128)(2,1)S(1)} %pad.4) | data formatting | bytes 1351680 | tf_op jit(solution)/shard_map/conv_general_dilated | solution.py:23
  46.9 4.7 %copy.87 = bf16[64,20,1,8,33]{0,3,4,1,2:T(8,128)(2,1)} copy(bf16[64,20,1,8,33]{4,3,0,1,2:T(8,128)(2,1)} %reshape.216) | data formatting | bytes 1351680 | tf_op jit(solution)/shard_map/conv_general_dilated | solution.py:23
  51.6 0.9 slice.138
  52.5 4.5 %fusion.4 = (f32[18,8,33,64]{3,1,2,0:T(8,128)}, f32[18,8,33,64]{3,1,2,0:T(8,128)S(1)}) fusion(pred[8,33]{0,1:T(8,128)(4,1)S(1)} %copy-done.25, bf16[64,64,3,3]{1,0,3,2:T(8,128)(2,1)S(1)} %copy-done, bf16[64,20,1,7,2]{0,3,4,1,2:T(8,128)(2,1)S(1)} %slice.133, bf16[64,20,1,8,33]{0,3,4,1,2:T(8,128)(2,1)S(1)} %copy-done.7), kind=kOutput, calls=%fused_computation.8 | convolution fusion | flops 354026496 | bytes 3218696 | tf_op jit(solution)/shard_map/conv_general_dilated | solution.py:23
  57.0 3.7 %select_multiply_fusion = f32[18,8,33,64]{3,1,2,0:T(8,128)} fusion(f32[18,8,33,64]{3,1,2,0:T(8,128)S(1)} %get-tuple-element.27, bf16[64,64,3,3]{1,0,3,2:T(8,128)(2,1)S(1)} %copy-done.24, bf16[64,20,1,7,2]{0,3,4,1,2:T(8,128)(2,1)S(1)} %slice.138, bf16[64,20,1,8,33]{0,3,4,1,2:T(8,128)(2,1)S(1)} %copy-done.8, pred[8,33]{0,1:T(8,128)(4,1)S(1)} %copy-done.25), kind=kOutput, calls=%fused_computation.6 | convolution fusion | flops 355547136 | bytes 3218696 | tf_op jit(solution)/shard_map/conv_general_dilated | solution.py:23
  60.8 5.2 %copy.127 = f32[18,8,33,64]{2,1,3,0:T(8,128)} copy(f32[18,8,33,64]{3,1,2,0:T(8,128)} %select_multiply_fusion) | data formatting | bytes 2433024 | tf_op jit(solution)/shard_map/mul | solution.py:91
  65.9 3.9 %reshape.213 = f32[18,1,264,64]{2,3,0,1:T(8,128)S(1)} reshape(f32[18,8,33,64]{2,1,3,0:T(8,128)} %copy.127) | data formatting | bytes 2433024 | tf_op jit(solution)/shard_map/mul | solution.py:91
  69.8 5.1 %copy.126 = f32[18,8,33,64]{2,1,3,0:T(8,128)} copy(f32[18,8,33,64]{3,1,2,0:T(8,128)} %get-tuple-element.26) | data formatting | bytes 2433024 | tf_op jit(solution)/shard_map/jit(silu)/mul | solution.py:86
  74.9 5.0 %reshape.212 = f32[18,1,264,64]{2,3,0,1:T(8,128)} reshape(f32[18,8,33,64]{2,1,3,0:T(8,128)} %copy.126) | data formatting | bytes 2433024 | tf_op jit(solution)/shard_map/jit(silu)/mul | solution.py:86
  79.9 3.4 %fusion.83 = (bf16[1,64,18,258]{3,1,2,0:T(8,128)(2,1)S(1)}, bf16[64,18,1,258]{3,0,1,2:T(8,128)(2,1)}, bf16[64,18,1,258]{3,0,1,2:T(8,128)(2,1)S(1)}, bf16[1,64,18,258]{3,1,2,0:T(8,128)(2,1)}) fusion(f32[18,258]{1,0:T(8,128)S(1)} %and_convert_fusion, f32[18,1,264,64]{2,3,0,1:T(8,128)} %reshape.212, f32[18,1,264,64]{2,3,0,1:T(8,128)S(1)} %reshape.213), kind=kLoop, calls=%fused_computation.124 | loop fusion | flops 1188864 | bytes 4774032 | tf_op jit(solution)/shard_map/convert_element_type | solution.py:86
  83.3 1.0 convolution_bitcast_fusion.3
  84.4 1.0 convolution_bitcast_fusion.4
  85.4 0.9 convolution_bitcast_fusion.5
  86.3 1.0 convolution_bitcast_fusion.6
  87.4 1.0 convolution_bitcast_fusion.7
  88.4 0.9 convolution_bitcast_fusion.8
  89.3 1.0 convolution_bitcast_fusion
  90.4 1.0 convolution_bitcast_fusion.1
  91.4 0.9 convolution_bitcast_fusion.2
  92.3 1.1 pad.6
  93.4 3.5 %reshape.217 = bf16[64,18,1,8,33]{4,3,0,1,2:T(8,128)(2,1)S(1)} reshape(bf16[64,18,1,264]{3,0,1,2:T(8,128)(2,1)} %pad.6) | data formatting | bytes 1216512 | tf_op jit(solution)/shard_map/conv_general_dilated | solution.py:23
  96.9 2.7 %copy.92 = bf16[64,18,1,8,33]{0,3,4,1,2:T(8,128)(2,1)} copy(bf16[64,18,1,8,33]{4,3,0,1,2:T(8,128)(2,1)S(1)} %reshape.217) | data formatting | bytes 1216512 | tf_op jit(solution)/shard_map/conv_general_dilated | solution.py:23
  99.6 0.9 slice.140
  100.5 2.9 %select_convert_fusion = bf16[16,8,33,64]{3,1,2,0:T(8,128)(2,1)S(1)} fusion(bf16[64,64,3,3]{1,0,3,2:T(8,128)(2,1)S(1)} %copy-done, bf16[64,18,1,7,2]{0,3,4,1,2:T(8,128)(2,1)S(1)} %slice.140, bf16[64,18,1,8,33]{0,3,4,1,2:T(8,128)(2,1)} %copy.92, pred[8,33]{0,1:T(8,128)(4,1)} %constant.49), kind=kOutput, calls=%fused_computation.9 | convolution fusion | flops 313903104 | bytes 1255176 | tf_op jit(solution)/shard_map/conv_general_dilated | solution.py:23
  103.8 2.2 copy.116
  106.0 1.0 pad.2
  107.0 3.5 %reshape.215 = bf16[64,18,1,8,33]{4,3,0,1,2:T(8,128)(2,1)S(1)} reshape(bf16[64,18,1,264]{3,0,1,2:T(8,128)(2,1)} %pad.2) | data formatting | bytes 1216512 | tf_op jit(solution)/shard_map/conv_general_dilated | solution.py:23
  110.5 2.7 %copy.83 = bf16[64,18,1,8,33]{0,3,4,1,2:T(8,128)(2,1)} copy(bf16[64,18,1,8,33]{4,3,0,1,2:T(8,128)(2,1)S(1)} %reshape.215) | data formatting | bytes 1216512 | tf_op jit(solution)/shard_map/conv_general_dilated | solution.py:23
  113.2 0.9 slice.135
  114.1 4.0 %select_convert_fusion.1 = bf16[16,8,33,64]{3,1,2,0:T(8,128)(2,1)S(1)} fusion(bf16[64,64,3,3]{1,0,3,2:T(8,128)(2,1)} %param.6, bf16[64,18,1,7,2]{0,3,4,1,2:T(8,128)(2,1)S(1)} %slice.135, bf16[64,18,1,8,33]{0,3,4,1,2:T(8,128)(2,1)} %copy.83, pred[8,33]{0,1:T(8,128)(4,1)} %constant.49), kind=kOutput, calls=%fused_computation.10 | convolution fusion | flops 313903104 | bytes 1255176 | tf_op jit(solution)/shard_map/conv_general_dilated | solution.py:23
  118.4 0.9 copy-done.1
  119.3 0.4 fusion.80
  119.9 0.7 pad_maximum_fusion.15
  120.6 0.6 fusion.37
  121.2 0.6 fusion.45
  121.8 0.3 fusion.41
  122.2 0.6 fusion.48
  122.8 0.6 fusion.55
  123.4 0.6 fusion.62
  124.0 0.6 fusion.73
  124.5 0.3 fusion.70
  124.9 0.7 pad_maximum_fusion.14
  125.9 2.2 copy.115
  128.0 126.1 %all-reduce.3.cloned.1.call-done = (f32[64,64,3,3]{1,0,3,2:T(8,128)}, f32[64,64,3,3]{1,0,3,2:T(8,128)}) async-done(((f32[64,64,3,3]{1,0,3,2:T(8,128)}, f32[64,64,3,3]{1,0,3,2:T(8,128)}), (f32[64,64,3,3]{1,0,3,2:T(8,128)}, f32[64,64,3,3]{1,0,3,2:T(8,128)})) %all-reduce.3.cloned.1.call-update) | async-done | bytes 294928 | tf_op jit(solution)/shard_map/psum | solution.py:95
  254.1 1.7 broadcast_multiply_fusion
  255.8 1.7 broadcast_multiply_fusion.1
  (70 shorter events, 1.9 us)
Async XLA Ops:
  7.2 45.3 %copy-start = (bf16[64,64,3,3]{1,0,3,2:T(8,128)(2,1)S(1)}, bf16[64,64,3,3]{1,0,3,2:T(8,128)(2,1)}, u32[]{:S(2)}) copy-start(bf16[64,64,3,3]{1,0,3,2:T(8,128)(2,1)} %param.5) | copy-start | bytes 221188
  7.2 246.9 %all-reduce.3.cloned.1.call-start = ((), (), s32[]{:S(2)}) async-start(), calls=%async_computation | async-start | bytes 1179648 | tf_op jit(solution)/shard_map/psum | solution.py:95
  9.7 7.6 %collective-permute-start = (bf16[1,128,2,256]{3,1,2,0:T(8,128)(2,1)S(1)}, bf16[1,128,2,256]{3,1,2,0:T(8,128)(2,1)S(1)}, u32[]{:S(2)}, u32[]{:S(2)}) collective-permute-start(bf16[1,128,2,256]{3,1,2,0:T(8,128)(2,1)S(1)} %get-tuple-element.22), channel_id=1, source_target_pairs={{0,4},{1,5},{2,6},{3,7},{8,12},{9,13},{10,14},{11,15},{16,20},{17,... | collective-permute-start | bytes 393224 | tf_op jit(solution)/shard_map/ppermute | solution.py:16
  14.6 6.9 %collective-permute-start.1 = (bf16[1,128,2,256]{3,1,2,0:T(8,128)(2,1)S(1)}, bf16[1,128,2,256]{3,1,2,0:T(8,128)(2,1)S(1)}, u32[]{:S(2)}, u32[]{:S(2)}) collective-permute-start(bf16[1,128,2,256]{3,1,2,0:T(8,128)(2,1)S(1)} %get-tuple-element.23), channel_id=1, source_target_pairs={{4,0},{5,1},{6,2},{7,3},{12,8},{13,9},{14,10},{15,11},{20,16},{21,... | collective-permute-start | bytes 393224 | tf_op jit(solution)/shard_map/ppermute | solution.py:17
  17.3 14.7 %copy-start.9 = (bf16[1,128,2,256]{3,1,2,0:T(8,128)(2,1)}, bf16[1,128,2,256]{3,1,2,0:T(8,128)(2,1)S(1)}, u32[]{:S(2)}) copy-start(bf16[1,128,2,256]{3,1,2,0:T(8,128)(2,1)S(1)} %collective-permute-done) | copy-start | bytes 393220
  21.4 10.5 %copy-start.11 = (bf16[1,128,2,256]{3,1,2,0:T(8,128)(2,1)}, bf16[1,128,2,256]{3,1,2,0:T(8,128)(2,1)S(1)}, u32[]{:S(2)}) copy-start(bf16[1,128,2,256]{3,1,2,0:T(8,128)(2,1)S(1)} %collective-permute-done.1) | copy-start | bytes 393220
  22.2 5.1 %collective-permute-start.2 = (bf16[1,128,20,2]{1,3,2,0:T(2,128)(2,1)S(1)}, bf16[1,128,20,2]{1,3,2,0:T(2,128)(2,1)S(1)}, u32[]{:S(2)}, u32[]{:S(2)}) collective-permute-start(bf16[1,128,20,2]{1,3,2,0:T(2,128)(2,1)S(1)} %copy.72), channel_id=1, source_target_pairs={{0,1},{1,2},{2,3},{4,5},{5,6},{6,7},{8,9},{9,10},{10,11},{12,13},{... | collective-permute-start | bytes 30728 | tf_op jit(solution)/shard_map/ppermute | solution.py:16
  26.0 5.6 %collective-permute-start.3 = (bf16[1,128,20,2]{1,3,2,0:T(2,128)(2,1)S(1)}, bf16[1,128,20,2]{1,3,2,0:T(2,128)(2,1)S(1)}, u32[]{:S(2)}, u32[]{:S(2)}) collective-permute-start(bf16[1,128,20,2]{1,3,2,0:T(2,128)(2,1)S(1)} %copy.73), channel_id=1, source_target_pairs={{1,0},{2,1},{3,2},{5,4},{6,5},{7,6},{9,8},{10,9},{11,10},{13,12},{... | collective-permute-start | bytes 30728 | tf_op jit(solution)/shard_map/ppermute | solution.py:17
  27.8 6.3 %copy-start.3 = (bf16[1,128,20,2]{3,1,2,0:T(8,128)(2,1)}, bf16[1,128,20,2]{3,1,2,0:T(8,128)(2,1)S(1)}, u32[]{:S(2)}) copy-start(bf16[1,128,20,2]{3,1,2,0:T(8,128)(2,1)S(1)} %copy.74) | copy-start | bytes 30724
  32.0 0.9 copy-start.5
  46.8 5.7 %copy-start.7 = (bf16[64,20,1,8,33]{0,3,4,1,2:T(8,128)(2,1)S(1)}, bf16[64,20,1,8,33]{0,3,4,1,2:T(8,128)(2,1)}, u32[]{:S(2)}) copy-start(bf16[64,20,1,8,33]{0,3,4,1,2:T(8,128)(2,1)} %copy.78) | copy-start | bytes 2027524
  46.8 5.7 %copy-start.25 = (pred[8,33]{0,1:T(8,128)(4,1)S(1)}, pred[8,33]{0,1:T(8,128)(4,1)}, u32[]{:S(2)}) copy-start(pred[8,33]{0,1:T(8,128)(4,1)} %constant.50) | copy-start | bytes 796
  52.5 4.5 %copy-start.8 = (bf16[64,20,1,8,33]{0,3,4,1,2:T(8,128)(2,1)S(1)}, bf16[64,20,1,8,33]{0,3,4,1,2:T(8,128)(2,1)}, u32[]{:S(2)}) copy-start(bf16[64,20,1,8,33]{0,3,4,1,2:T(8,128)(2,1)} %copy.87) | copy-start | bytes 2027524
  52.5 4.5 %copy-start.24 = (bf16[64,64,3,3]{1,0,3,2:T(8,128)(2,1)S(1)}, bf16[64,64,3,3]{1,0,3,2:T(8,128)(2,1)}, u32[]{:S(2)}) copy-start(bf16[64,64,3,3]{1,0,3,2:T(8,128)(2,1)} %param.6) | copy-start | bytes 221188
  79.9 3.4 %copy-start.13 = (bf16[1,64,16,256]{3,2,1,0:T(8,128)(2,1)S(1)}, bf16[1,64,16,256]{3,2,1,0:T(8,128)(2,1)}, u32[]{:S(2)}) copy-start(bf16[1,64,16,256]{3,2,1,0:T(8,128)(2,1)} %param.7) | copy-start | bytes 1572868
  103.6 2.4 copy-start.2
  114.1 4.3 %copy-start.14 = (bf16[1,64,16,256]{3,2,1,0:T(8,128)(2,1)S(1)}, bf16[1,64,16,256]{3,2,1,0:T(8,128)(2,1)}, u32[]{:S(2)}) copy-start(bf16[1,64,16,256]{3,2,1,0:T(8,128)(2,1)} %param.4) | copy-start | bytes 1572868
  118.2 1.2 copy-start.1
  118.2 1.6 copy-start.21
  118.2 1.6 copy-start.22
  118.2 1.6 copy-start.23
  118.2 1.6 copy-start.15
  118.2 1.6 copy-start.16
  118.2 1.6 copy-start.17
  118.2 1.6 copy-start.18
  118.2 1.6 copy-start.19
  118.2 1.6 copy-start.20
  118.3 2.4 copy-start.6
  118.3 2.4 copy-start.10
  118.3 2.4 copy-start.12
  119.8 1.5 copy-start.4
Sparse Core Ops, SparseCore 0:
  125.8 128.2 all-reduce.2
where the time goes:
time: 265 us; the launch traced here: 264 us
  waiting for transfers between devices  135 us (51%)
  local copies, waits for them, and re-layouts  64.7 us (24%)
  matrix products  28.8 us (11%)
  between operations  14.6 us (6%)
  starting transfers between devices  11 us (4%)
  other arithmetic  9.86 us (4%)
    psum x1, waiting for transfers between devices, on_device(): lax.psum((first_grad, second_grad), ('dp', 'row', 'col'))  126 us
    conv_general_dilated x12, local copies, waits for them, and re-layouts, convolve(): lax.conv_general_dilated(padded, kernel, (1, 1), 'VALID', dimension_numbe...  32.1 us
    conv_general_dilated x4, matrix products, convolve(): lax.conv_general_dilated(padded, kernel, (1, 1), 'VALID', dimension_numbe...  15.2 us
    dot_general x18, matrix products, kernel_grad(): jnp.einsum('nihw,nohw->oi', window, upstream, preferred_element_type=jnp....  13.6 us
    mul x2, local copies, waits for them, and re-layouts, on_device(): act_padded = (jax.nn.silu(hidden) * inside).astype(jnp.bfloat16)  10.1 us
    mul x2, local copies, waits for them, and re-layouts, on_device(): hid_padded = (act_grad * silu_grad(hidden) * inside).astype(jnp.bfloat16)  9 us
    ppermute x2, starting transfers between devices, extended(): before = lax.ppermute(last, axis, up)  8.36 us
    ppermute x2, waiting for transfers between devices, extended(): after = lax.ppermute(leading, axis, down)  7.89 us
  transfers between devices with their start and end apart: 5, of which 4 were waited for; matrix products, arithmetic and copies ran while one was open for 1% of the time, Pallas kernels for 0%

commit v1 on v0

v1 whole, which is shorter than its diff:
```python
import functools
import math

import jax
import jax.numpy as jnp
from jax import lax
from jax.experimental import pallas as pl
from jax.experimental.pallas import tpu as pltpu
from jax.sharding import PartitionSpec as P

BF = jnp.bfloat16
F32 = jnp.float32
LANES = 128
SLOT = 32
PIECES = 2


def kernel_call(body, outs, scratch=(), flops=0, name=None, **more):
    return pl.pallas_call(
        body,
        out_shape=outs,
        **more,
        scratch_shapes=list(scratch),
        cost_estimate=pl.CostEstimate(flops=flops, transcendentals=0, bytes_accessed=1 << 20),
        compiler_params=pltpu.CompilerParams(vmem_limit_bytes=24 << 20),
        name=name,
    )


def lanes_of(shape):
    return lax.broadcasted_iota(jnp.int32, shape, len(shape) - 1)


def pairs(size, second):
    start = 1 if second else 0
    out = []
    for i in range(start, size - 1, 2):
        out += [(i, i + 1), (i + 1, i)]
    return out


def swap(array, axis, second):
    perm = pairs(lax.axis_size(axis), second)
    if not perm:
        return None
    return lax.ppermute(array, axis, perm)


def pack_body(
    img, cot, k1, k2, x16, own, taps1, taps2, send_a, send_b, row_a, row_b,
    staged, wide, sems, tap_sems,
):
    ch, rows, cols = img.shape[1:]
    halves = cols // LANES
    pitch = wide.shape[2] // ch
    col_odd = lax.axis_index("col") % 2 == 1
    row_odd = lax.axis_index("row") % 2 == 1
    lane = lanes_of((ch, LANES))
    cut = ch // PIECES
    tap_copies = [
        pltpu.make_async_copy(src, dst, tap_sems.at[k])
        for k, (src, dst) in enumerate(((k1, taps1), (k2, taps2)))
    ]
    for copy in tap_copies:
        copy.start()
    copies = []
    for which, ref in enumerate((img, cot)):
        for k in range(PIECES):
            span = pl.ds(k * cut, cut)
            copy = pltpu.make_async_copy(
                ref.at[0, span], staged.at[which, span], sems.at[which, k]
            )
            copy.start()
            copies.append(copy)
    for which in range(2):
        base = which * ch
        left = jnp.zeros((ch, LANES), F32)
        right = jnp.zeros((ch, LANES), F32)
        for k in range(PIECES):
            copies[which * PIECES + k].wait()
            for c in range(k * cut, (k + 1) * cut):
                for half in range(halves):
                    wide[which, half, c * pitch : c * pitch + rows, :] = staged[
                        which, c, :, half * LANES : (half + 1) * LANES
                    ].astype(F32)
        for half in range(halves):
            for h in range(rows):
                v = wide[which, half, pl.ds(h, ch, stride=pitch), :]
                x16[h, base : base + ch, half * LANES : (half + 1) * LANES] = v.astype(BF)
                for j in range(2):
                    at = j * SLOT + h + 2
                    if half == 0:
                        left = jnp.where(lane == at, pltpu.roll(v, (at - j) % LANES, 1), left)
                    if half == halves - 1:
                        src = LANES - 2 + j
                        right = jnp.where(lane == at, pltpu.roll(v, (at - src) % LANES, 1), right)
        own[0, base : base + ch, :] = left.astype(BF)
        own[1, base : base + ch, :] = right.astype(BF)
        send_a[base : base + ch, :] = jnp.where(col_odd, left, right).astype(BF)
        send_b[base : base + ch, :] = jnp.where(col_odd, right, left).astype(BF)
    row_a[...] = x16[pl.ds(jnp.where(row_odd, 0, rows - 2), 2)]
    if row_b is not None:
        row_b[...] = x16[pl.ds(jnp.where(row_odd, rows - 2, 0), 2)]
    for copy in tap_copies:
        copy.wait()


def sides(a, b, odd):
    zero = jnp.zeros(a.shape, a.dtype)
    b = zero if b is None else b
    return jnp.where(odd, a, b), jnp.where(odd, b, a)


def corner_body(rows, strip_a, strip_b, send_a, send_b):
    col_odd = lax.axis_index("col") % 2 == 1
    row_odd = lax.axis_index("row") % 2 == 1
    lane = lanes_of(strip_a.shape)
    west, east = sides(
        strip_a[...].astype(F32), None if strip_b is None else strip_b[...].astype(F32), col_odd
    )
    both = jnp.where(lane < 2 * SLOT, west, pltpu.roll(east, 2 * SLOT, 1))
    slot = lane % SLOT
    down = jnp.where(slot < 2, pltpu.roll(both, (-rows) % LANES, 1), 0.0)
    up = jnp.where((slot >= rows + 2) & (slot < rows + 4), pltpu.roll(both, rows, 1), 0.0)
    send_a[...] = jnp.where(row_odd, up, down).astype(BF)
    if send_b is not None:
        send_b[...] = jnp.where(row_odd, down, up).astype(BF)


def put_shifted(dst, at, half_values, edge, first, last):
    ch = half_values[0].shape[0]
    n = len(half_values)
    fwd = [pltpu.roll(v, 1, 1) for v in half_values]
    back = [pltpu.roll(v, LANES - 1, 1) for v in half_values]
    for k in range(n):
        at_lanes = slice(k * LANES, (k + 1) * LANES)
        before = edge if k == 0 else fwd[k - 1]
        after = edge if k == n - 1 else back[k + 1]
        dst[at, 0:ch, at_lanes] = jnp.where(first, before, fwd[k]).astype(BF)
        dst[at, ch : 2 * ch, at_lanes] = half_values[k].astype(BF)
        dst[at, 2 * ch : 3 * ch, at_lanes] = jnp.where(last, after, back[k]).astype(BF)


def halves_of(v):
    return [v[:, k * LANES : (k + 1) * LANES] for k in range(v.shape[1] // LANES)]


def has_neighbours():
    out = []
    for axis in ("row", "col"):
        at, size = lax.axis_index(axis), lax.axis_size(axis)
        out += [jnp.where(at > 0, 1.0, 0.0), jnp.where(at < size - 1, 1.0, 0.0)]
    return out


def side_strips(strip_a, strip_b):
    return sides(
        strip_a[...].astype(F32),
        None if strip_b is None else strip_b[...].astype(F32),
        lax.axis_index("col") % 2 == 1,
    )


def edge_of(before, behind, lane_before, lane_behind):
    near = lanes_of(before.shape) < LANES // 2
    return jnp.where(
        near,
        pltpu.roll(before, (-lane_before) % LANES, 1),
        pltpu.roll(behind, (LANES - 1 - lane_behind) % LANES, 1),
    )


def border(weights, west, east, left, right):
    e0 = lanes_of(west.shape) < SLOT
    b0 = jnp.where(e0, west, right)
    b1 = jnp.where(e0, pltpu.roll(west, LANES - SLOT, 1), pltpu.roll(east, SLOT, 1))
    b2 = jnp.where(e0, left, east)
    taps = []
    for a in range(3):
        taps += [pltpu.roll(b, (1 - a) % LANES, 1) if a != 1 else b for b in (b0, b1, b2)]
    stack = jnp.concatenate(taps, 0).astype(BF)
    return jnp.dot(weights, stack, preferred_element_type=F32)


def activation(hidden, act_grad):
    s = 0.5 * jnp.tanh(0.5 * hidden) + 0.5
    return hidden * s, act_grad * (s * (1.0 + hidden * (1.0 - s)))


def row_weights(dst, kernel, flip):
    ch = kernel.shape[2]
    zero = jnp.zeros((ch, ch), BF)
    taps = []
    for a in range(3):
        for b in range(3):
            taps.append(kernel[2 - a, 2 - b].T if flip else kernel[a, b])
    for p in range(2):
        blocks = [zero] * (3 * p) + taps + [zero] * (3 - 3 * p)
        for k in range(6):
            dst[p * ch : (p + 1) * ch, k * LANES : (k + 1) * LANES] = jnp.concatenate(
                blocks[2 * k : 2 * k + 2], 1
            )


NT = (((1,), (1,)), ((), ()))


def add_grads(sums, lhs_rows, rhs):
    lhs = jnp.concatenate(lhs_rows, 0)
    return sums + lax.dot_general(lhs, rhs, NT, preferred_element_type=F32)


def inner_body(
    taps1, taps2, x16, own, strip_a, strip_b,
    xi, xc, acts, hids, g1_out, g2_out, wf,
):
    rows, ch2, cols = x16.shape
    ch = ch2 // 2
    row_weights(wf.at[0], taps1, False)
    row_weights(wf.at[1], taps2, True)
    west, east = side_strips(strip_a, strip_b)
    left, right = own[0].astype(F32), own[1].astype(F32)
    first = lanes_of((ch, LANES)) == 0
    last = lanes_of((ch, LANES)) == LANES - 1
    west_b, east_b = west.astype(BF), east.astype(BF)
    for h in range(rows):
        edge = edge_of(west_b, east_b, SLOT + h + 2, h + 2)
        for which, dst in enumerate((xi, xc)):
            s = slice(which * ch, (which + 1) * ch)
            put_shifted(dst, h, halves_of(x16[h, s]), edge[s], first, last)
    lane = lanes_of((ch, LANES))
    _, _, has_west, has_east = has_neighbours()
    keep = jnp.where(lane < SLOT, has_west, has_east) > 0.0
    sides_of = lambda s: (west[s], east[s], left[s], right[s])
    act_e, hid_e = activation(
        border(wf[0, :ch, : 9 * ch], *sides_of(slice(0, ch))),
        border(wf[1, :ch, : 9 * ch], *sides_of(slice(ch, ch2))),
    )
    act_e = jnp.where(keep, act_e, 0.0).astype(BF)
    hid_e = jnp.where(keep, hid_e, 0.0).astype(BF)
    zero_row = jnp.zeros((ch, cols), BF)
    for t in range((rows - 2) // 2):
        at = 2 * t
        hidden = jnp.dot(
            wf[0], xi[at : at + 4].reshape(12 * ch, cols), preferred_element_type=F32
        )
        act_grad = jnp.dot(
            wf[1], xc[at : at + 4].reshape(12 * ch, cols), preferred_element_type=F32
        )
        for values, dst, e in zip(activation(hidden, act_grad), (acts, hids), (act_e, hid_e)):
            for p in range(2):
                h = at + p + 1
                put_shifted(
                    dst, at + p, halves_of(values[p * ch : (p + 1) * ch].astype(BF)),
                    edge_of(e, e, h + 2, SLOT + h + 2), first, last,
                )
    g1 = jnp.zeros((3 * ch, 3 * ch), F32)
    for r in range(rows):
        lhs = [
            hids[h - 1, ch : 2 * ch] if 1 <= h <= rows - 2 else zero_row for h in range(r - 1, r + 2)
        ]
        g1 = add_grads(g1, lhs, xi[r])
    g1_out[...] = g1
    g2 = jnp.zeros((3 * ch, 3 * ch), F32)
    for r in range(1, rows - 1):
        g2 = add_grads(g2, [x16[h, ch:] for h in range(r - 1, r + 2)], acts[r - 1])
    g2_out[...] = g2


def outer_body(
    wf, x16, own, xi, xc, hids, g1_in, g2_in,
    strip_a, strip_b, row_a, row_b, corner_a, corner_b,
    acts_o, hids_o, mine, other, xo, grads,
):
    rows, ch2, cols = x16.shape
    ch = ch2 // 2
    has_north, has_south, has_west, has_east = has_neighbours()
    lane2 = lanes_of((ch2, LANES))
    west, east = side_strips(strip_a, strip_b)
    corner = corner_a[...].astype(F32)
    if corner_b is not None:
        corner = corner + corner_b[...].astype(F32)
    west = west + jnp.where(lane2 < 2 * SLOT, corner, 0.0)
    east = east + jnp.where(lane2 < 2 * SLOT, pltpu.roll(corner, LANES - 2 * SLOT, 1), 0.0)
    north, south = sides(
        row_a[...], None if row_b is None else row_b[...], lax.axis_index("row") % 2 == 1
    )
    left, right = own[0].astype(F32), own[1].astype(F32)
    first = lanes_of((ch, LANES)) == 0
    last = lanes_of((ch, LANES)) == LANES - 1
    west_b, east_b = west.astype(BF), east.astype(BF)
    for k in range(4):
        slot = k if k < 2 else rows + k
        row = (north if k < 2 else south)[k % 2]
        lo, hi = row[:, :LANES].astype(F32), row[:, cols - LANES :].astype(F32)
        left = jnp.where(lane2 == slot, pltpu.roll(lo, slot, 1), left)
        right = jnp.where(
            lane2 == SLOT + slot, pltpu.roll(hi, (SLOT + slot - LANES + 1) % LANES, 1), right
        )
        edge = edge_of(west_b, east_b, SLOT + slot, slot)
        for which in range(2):
            s = slice(which * ch, (which + 1) * ch)
            put_shifted(xo.at[which], k, halves_of(row[s]), edge[s], first, last)
    lane = lanes_of((ch, LANES))
    slots = lane % SLOT
    keep = jnp.where(lane < SLOT, has_west, has_east)
    keep = keep * jnp.where(slots == 1, has_north, 1.0) * jnp.where(slots == rows + 2, has_south, 1.0)
    sides_of = lambda s: (west[s], east[s], left[s], right[s])
    act_e, hid_e = activation(
        border(wf[0, :ch, : 9 * ch], *sides_of(slice(0, ch))),
        border(wf[1, :ch, : 9 * ch], *sides_of(slice(ch, ch2))),
    )
    act_e = jnp.where(keep > 0.0, act_e, 0.0).astype(BF)
    hid_e = jnp.where(keep > 0.0, hid_e, 0.0).astype(BF)
    for t in range(2):
        stacks = []
        for which, mid in enumerate((xi, xc)):
            ends = xo[which, 2 * t : 2 * t + 2].reshape(6 * ch, cols)
            if t == 0:
                stack = [ends, mid[0:2].reshape(6 * ch, cols)]
            else:
                stack = [mid[rows - 2 : rows].reshape(6 * ch, cols), ends]
            stacks.append(jnp.concatenate(stack, 0))
        hidden = jnp.dot(wf[0], stacks[0], preferred_element_type=F32)
        act_grad = jnp.dot(wf[1], stacks[1], preferred_element_type=F32)
        for values, dst, e in zip(activation(hidden, act_grad), (acts_o, hids_o), (act_e, hid_e)):
            for p in range(2):
                at = 2 * t + p
                h = at - 1 if t == 0 else rows - 3 + at
                v = values[p * ch : (p + 1) * ch]
                if at == 0:
                    v = jnp.where(has_north > 0.0, v, 0.0)
                if at == 3:
                    v = jnp.where(has_south > 0.0, v, 0.0)
                put_shifted(
                    dst, at, halves_of(v.astype(BF)), edge_of(e, e, h + 2, SLOT + h + 2), first, last
                )
    zero_row = jnp.zeros((ch, cols), BF)
    g1, g2 = g1_in[...], g2_in[...]
    for k, r in ((0, -1), (1, 0), (2, rows - 1), (3, rows)):
        lhs = [x16[h, ch:] if 0 <= h < rows else zero_row for h in range(r - 1, r + 2)]
        g2 = add_grads(g2, lhs, acts_o[k])
    for h, row in ((0, hids_o[1, ch : 2 * ch]), (rows - 1, hids_o[2, ch : 2 * ch])):
        for r in range(h - 1, h + 2):
            rhs = xi[r] if 0 <= r < rows else xo[0, 1 if r < 0 else 2]
            lhs = [row if h == r - 1 + k else zero_row for k in range(3)]
            g1 = add_grads(g1, lhs, rhs)
    grads[0 : 3 * ch, :] = g1[:, : 2 * ch]
    grads[3 * ch : 6 * ch, :] = g2[:, : 2 * ch]
    grads[6 * ch : 9 * ch, :] = jnp.concatenate([g1[:, 2 * ch :], g2[:, 2 * ch :]], 1)
    count = mine.shape[0]
    core = lax.axis_index("dp") % 2
    mine[...] = grads[pl.ds(core * count, count), :]
    other[...] = grads[pl.ds((1 - core) * count, count), :]


def back_body(flip, kernel, mid, ends, out, weights, wide):
    rows = mid.shape[0] + 2
    ch = kernel.shape[2]
    cols = mid.shape[2]
    pitch = wide.shape[1] // ch
    row_weights(weights, kernel, flip)
    for t in range(rows // 2):
        if t == 0:
            stack = jnp.concatenate([ends[0:2], mid[0:2]], 0)
        elif t == rows // 2 - 1:
            stack = jnp.concatenate([mid[rows - 4 : rows - 2], ends[2:4]], 0)
        else:
            stack = mid[2 * t - 2 : 2 * t + 2]
        y = jnp.dot(weights[...], stack.reshape(12 * ch, cols), preferred_element_type=F32)
        for p in range(2):
            for half, part in enumerate(halves_of(y[p * ch : (p + 1) * ch])):
                wide[half, pl.ds(2 * t + p, ch, stride=pitch), :] = part
    for half in range(cols // LANES):
        for c in range(ch):
            out[0, c, :, half * LANES : (half + 1) * LANES] = wide[
                half, c * pitch : c * pitch + rows, :
            ].astype(BF)


def finish_body(factor, mine, other, first, second):
    core = lax.axis_index("dp") % 2
    m, o = mine[...].astype(F32) * factor, other[...].astype(F32) * factor
    whole = jnp.concatenate([jnp.where(core == 0, m, o), jnp.where(core == 0, o, m)], 0)
    ch = first.shape[2]
    tail = whole[6 * ch :]
    swapped = pltpu.roll(whole, LANES - ch, 1)
    for k, dst in ((0, first), (1, second)):
        for a in range(3):
            src = (2 - a) * ch
            dst[a, 0] = whole[k * 3 * ch + src : k * 3 * ch + src + ch, :ch]
            dst[a, 1] = swapped[k * 3 * ch + src : k * 3 * ch + src + ch, :ch]
            third = tail if k == 0 else swapped[6 * ch :]
            dst[a, 2] = third[src : src + ch, :ch]


def exchange(half, dims):
    axes = ("dp", "row", "col")
    sizes = [lax.axis_size(a) for a in axes]
    sent = half.astype(BF)
    total = sent.astype(F32)
    for pick in range(1, 1 << len(dims)):
        flips = [0, 0, 0]
        for k, (axis, bit) in enumerate(dims):
            if pick >> k & 1:
                flips[axis] ^= bit
        perm = []
        for d in range(sizes[0]):
            for r in range(sizes[1]):
                for c in range(sizes[2]):
                    to = (d ^ flips[0], r ^ flips[1], c ^ flips[2])
                    perm.append(
                        ((d * sizes[1] + r) * sizes[2] + c, (to[0] * sizes[1] + to[1]) * sizes[2] + to[2])
                    )
        total = total + lax.ppermute(sent, axes, perm).astype(F32)
    return total


def on_device(images, first_kernel, second_kernel, cotangent):
    ch, rows, cols = images.shape[1:]
    n_row, n_col, n_dp = (lax.axis_size(a) for a in ("row", "col", "dp"))
    total = rows * cols * n_row * n_col * n_dp * images.shape[0]
    factor = 1.0 / math.sqrt(total)
    pitch = 24
    halves = cols // LANES
    two_rows = n_row > 2
    two_cols = n_col > 2
    sds = jax.ShapeDtypeStruct
    strip = sds((2 * ch, LANES), BF)
    row_pair = sds((2, 2 * ch, cols), BF)
    hbm = pl.BlockSpec(memory_space=pltpu.HBM)

    def optional(body, flags):
        def wrapped(*refs):
            refs = list(refs)
            return body(*[refs.pop(0) if keep else None for keep in flags], *refs)

        return wrapped

    k1 = first_kernel.transpose(2, 3, 0, 1)
    k2 = second_kernel.transpose(2, 3, 0, 1)
    pack = kernel_call(
        optional(pack_body, [True] * 11 + [two_rows]),
        [sds((rows, 2 * ch, cols), BF), sds((2, 2 * ch, LANES), BF)]
        + [sds(k1.shape, BF), sds(k2.shape, BF), strip, strip]
        + [row_pair] * (1 + two_rows),
        [
            pltpu.VMEM((2, ch, rows, cols), BF),
            pltpu.VMEM((2, halves, ch * pitch, LANES), F32),
            pltpu.SemaphoreType.DMA((2, PIECES)),
            pltpu.SemaphoreType.DMA((2,)),
        ],
        in_specs=[hbm] * 4,
        flops=1 << 27,
        name="pack",
    )
    x16, own, taps1, taps2, send_a, send_b, *row_sends = pack(
        *[pltpu.with_memory_space_constraint(v, pltpu.HBM) for v in (images, cotangent, k1, k2)]
    )
    strips = [swap(send_a, "col", False)]
    if two_cols:
        strips.append(swap(send_b, "col", True))
    got_rows = [swap(s, "row", k == 1) for k, s in enumerate(row_sends)]
    corner_sends = kernel_call(
        optional(functools.partial(corner_body, rows), [True, two_cols, True, two_rows]),
        [strip] * (1 + two_rows),
        name="corner",
    )(*strips)
    corners = [swap(s, "row", k == 1) for k, s in enumerate(corner_sends)]
    shifted = lambda n: sds((n, 3 * ch, cols), BF)
    sums = sds((3 * ch, 3 * ch), F32)
    xi, xc, acts, hids, g1, g2, wf = kernel_call(
        optional(inner_body, [True] * 5 + [two_cols]),
        [shifted(rows), shifted(rows), shifted(rows - 2), shifted(rows - 2), sums, sums]
        + [sds((2, 2 * ch, 12 * ch), BF)],
        flops=1 << 30,
        name="inner",
    )(taps1, taps2, x16, own, *strips)
    half = sds((9 * ch // 2, LANES), F32)
    acts_o, hids_o, mine, other = kernel_call(
        optional(outer_body, [True] * 8 + [True, two_cols] + [True, two_rows] * 2),
        [shifted(4), shifted(4), half, half],
        [pltpu.VMEM((2, 4, 3 * ch, cols), BF), pltpu.VMEM((9 * ch, LANES), F32)],
        flops=1 << 28,
        name="outer",
    )(wf, x16, own, xi, xc, hids, g1, g2, *strips, *got_rows, *corners)

    def back(kernel, mid, ends, flip, name):
        return kernel_call(
            functools.partial(back_body, flip),
            [sds(images.shape, BF)],
            [
                pltpu.VMEM((2 * ch, 12 * ch), BF),
                pltpu.VMEM((halves, ch * pitch, LANES), F32),
            ],
            flops=1 << 29,
            name=name,
        )(kernel, mid, ends)[0]

    partner = [(i, i ^ 1) for i in range(n_dp)]
    total_half = mine + lax.ppermute(other, "dp", partner)
    steps = [(0, 1 << k) for k in range(1, n_dp.bit_length() - 1)]
    steps += [(1, 1 << k) for k in range(n_row.bit_length() - 1)]
    steps += [(2, 1 << k) for k in range(n_col.bit_length() - 1)]
    out = back(taps2, acts, acts_o, False, "out")
    grad_in = back(taps1, hids, hids_o, True, "grad_in")
    stages = [steps[k : k + 2] for k in range(0, len(steps), 2)]
    for k, stage in enumerate(stages):
        total_half = exchange(total_half, stage)
        if k == len(stages) - 2:
            total_half, out = lax.optimization_barrier((total_half, out))
        if k == len(stages) - 1:
            total_half, grad_in = lax.optimization_barrier((total_half, grad_in))
    rest = lax.ppermute(total_half, "dp", partner)
    taps = sds((3, 3, ch, ch), F32)
    first, second = kernel_call(
        functools.partial(finish_body, factor), [taps, taps], name="finish"
    )(total_half, rest)
    return out, grad_in, first.transpose(2, 3, 0, 1), second.transpose(2, 3, 0, 1)


def solution(mesh):
    in_specs = (P("dp", None, "row", "col"), P(), P(), P("dp", None, "row", "col"))
    out_specs = (P("dp", None, "row", "col"), P("dp", None, "row", "col"), P(), P())
    return jax.shard_map(
        on_device, mesh=mesh, in_specs=in_specs, out_specs=out_specs, check_vma=False
    )
```

time: 265 us -> 37.2 us (0.14)
  waiting for transfers between devices: 135 us -> 8.11 us
  local copies, waits for them, and re-layouts: 64.7 us -> 0 us
  matrix products: 28.8 us -> 0 us
  between operations: 14.6 us -> 0.71 us
  Pallas kernels: 0 us -> 9.82 us
  other arithmetic: 9.86 us -> 0.1 us
  starting transfers between devices: 11 us -> 18.3 us
    psum x1 -> x0, waiting for transfers between devices: 126 us -> none  [on_device(): lax.psum((first_grad, second_grad), ('dp', 'row', 'col'))]
    conv_general_dilated x12 -> x0, local copies, waits for them, and re-layouts: 32.1 us -> none  [convolve(): lax.conv_general_dilated(padded, kernel, (1, 1), 'VALID', dimension_numbe...]
    mul x4 -> x0, local copies, waits for them, and re-layouts: 19.1 us -> none  [the longest x2 10.1 us: on_device(): act_padded = (jax.nn.silu(hidden) * inside).astype(jnp.bfloat16)]
    conv_general_dilated x4 -> x0, matrix products: 15.2 us -> none  [convolve(): lax.conv_general_dilated(padded, kernel, (1, 1), 'VALID', dimension_numbe...]
    dot_general x18 -> x0, matrix products: 13.6 us -> none  [kernel_grad(): jnp.einsum('nihw,nohw->oi', window, upstream, preferred_element_type=jnp....]
    pallas_call x0 -> x7, Pallas kernels: none -> 9.82 us  [the longest x2 3.18 us: back(): kernel_call(functools.partial(back_body, flip), [sds(images.shape, BF)],...]
    unnamed x55 -> x0, local copies, waits for them, and re-layouts: 7.4 us -> none
    ppermute x4 -> x12, starting transfers between devices: 10.9 us -> 18.3 us  [the longest x6 11.2 us: exchange(): total = total + lax.ppermute(sent, axes, perm).astype(F32)]
  transfers between devices with their start and end apart: 5 -> 12, of which waited for: 4 -> 7; matrix products, arithmetic and copies ran while one was open for 1% -> 0% of each run, Pallas kernels for 0% -> 16%
where the time goes in v1:
time: 37.2 us; the launch traced here: 37.1 us
  starting transfers between devices  18.3 us (49%)
  Pallas kernels  9.82 us (26%)
  waiting for transfers between devices  8.11 us (22%)
  between operations  0.71 us (2%)
    ppermute x6, starting transfers between devices, exchange(): total = total + lax.ppermute(sent, axes, perm).astype(F32)  11.2 us
    ppermute x4, starting transfers between devices, swap(): return lax.ppermute(array, axis, perm)  7 us
    ppermute x6, waiting for transfers between devices, exchange(): total = total + lax.ppermute(sent, axes, perm).astype(F32)  5.38 us
    pallas_call x2, Pallas kernels, back(): kernel_call(functools.partial(back_body, flip), [sds(images.shape, BF)],...  3.18 us
    pallas_call x1, Pallas kernels, on_device(): kernel_call(optional(inner_body, [True] * 5 + [two_cols]), [shifted(rows)...  2.42 us
    pallas_call x1, Pallas kernels, on_device(): pack(*[pltpu.with_memory_space_constraint(v, pltpu.HBM) for v in (images,...  1.95 us
    ppermute x1, waiting for transfers between devices, on_device(): total_half = mine + lax.ppermute(other, 'dp', partner)  1.36 us
    ppermute x1, waiting for transfers between devices, on_device(): rest = lax.ppermute(total_half, 'dp', partner)  1.36 us
  transfers between devices with their start and end apart: 12, of which 7 were waited for; matrix products, arithmetic and copies ran while one was open for 0% of the time, Pallas kernels for 16%

profile of v1, /device:TPU:0, one launch (start us, length us, event | category | flops | bytes accessed | tf_op | source)
XLA Modules:
  0.0 37.1 jit_solution(4150598023698512944)
XLA Ops:
  0.6 2.0 %pack.1 = (bf16[16,128,256]{2,1,0:T(8,128)(2,1)S(1)}, bf16[2,128,128]{2,1,0:T(8,128)(2,1)S(1)}, bf16[3,3,64,64]{3,2,1,0:T(8,128)(2,1)S(1)}, bf16[3,3,64,64]{3,2,...) custom-call(bf16[1,64,16,256]{3,2,1,0:T(8,128)(2,1)} %refs_0_.1, ...), custom_call_target="tpu_custom_call" | custom-call | flops 134217728 | bytes 1048576 | tf_op jit(solution)/shard_map/pack/pallas_call | solution.py:457
  2.6 3.1 %collective-permute-start = (bf16[128,128]{1,0:T(8,128)(2,1)S(1)}, bf16[128,128]{1,0:T(8,128)(2,1)S(1)}, u32[]{:S(2)}, u32[]{:S(2)}) collective-permute-start(bf16[128,128]{1,0:T(8,128)(2,1)S(1)} %get-tuple-element.32), channel_id=1, source_target_pairs={{0,1},{1,0},{2,3},{3,2},{4,5},{5,4},{6,7},{7,6},{8,9},{9,8},{10,11... | collective-permute-start | bytes 98312 | tf_op jit(solution)/shard_map/ppermute | solution.py:46
  5.7 0.7 %collective-permute-start.1 = (bf16[128,128]{1,0:T(8,128)(2,1)S(1)}, bf16[128,128]{1,0:T(8,128)(2,1)S(1)}, u32[]{:S(2)}, u32[]{:S(2)}) collective-permute-start(bf16[128,128]{1,0:T(8,128)(2,1)S(1)} %get-tuple-element.33), channel_id=1, source_target_pairs={{1,2},{2,1},{5,6},{6,5},{9,10},{10,9},{13,14},{14,13},{17,18},{18,... | collective-permute-start | bytes 98312 | tf_op jit(solution)/shard_map/ppermute | solution.py:46
  6.4 1.6 %collective-permute-start.2 = (bf16[2,128,256]{2,1,0:T(8,128)(2,1)S(1)}, bf16[2,128,256]{2,1,0:T(8,128)(2,1)S(1)}, u32[]{:S(2)}, u32[]{:S(2)}) collective-permute-start(bf16[2,128,256]{2,1,0:T(8,128)(2,1)S(1)} %get-tuple-element.40), channel_id=1, source_target_pairs={{0,4},{4,0},{1,5},{5,1},{2,6},{6,2},{3,7},{7,3},{8,12},{12,8},{9,1... | collective-permute-start | bytes 393224 | tf_op jit(solution)/shard_map/ppermute | solution.py:46
  7.9 0.0 collective-permute-done.refs_4_.refs_0_.refs_8_
  7.9 0.0 collective-permute-done.1.refs_5_.refs_1_.refs_9_
  7.9 0.2 corner.1
  8.1 1.7 %collective-permute-start.3 = (bf16[128,128]{1,0:T(8,128)(2,1)S(1)}, bf16[128,128]{1,0:T(8,128)(2,1)S(1)}, u32[]{:S(2)}, u32[]{:S(2)}) collective-permute-start(bf16[128,128]{1,0:T(8,128)(2,1)S(1)} %corner.1), channel_id=1, source_target_pairs={{0,4},{4,0},{1,5},{5,1},{2,6},{6,2},{3,7},{7,3},{8,12},{12,8},{9,1... | collective-permute-start | bytes 98312 | tf_op jit(solution)/shard_map/ppermute | solution.py:46
  9.8 2.4 %inner.1 = (bf16[16,192,256]{2,1,0:T(8,128)(2,1)S(1)}, bf16[16,192,256]{2,1,0:T(8,128)(2,1)S(1)}, bf16[14,192,256]{2,1,0:T(8,128)(2,1)S(1)}, bf16[14,192,256]{2,...) custom-call(bf16[3,3,64,64]{3,2,1,0:T(8,128)(2,1)S(1)} %get-tuple-element.28, ...), custom_call_target="tpu_custom_call" | custom-call | flops 1073741824 | bytes 1048576 | tf_op jit(solution)/shard_map/inner/pallas_call | solution.py:472
  12.2 0.0 collective-permute-done.3.refs_11_
  12.2 0.0 collective-permute-done.2.refs_10_
  12.2 1.2 %outer.1 = (bf16[4,192,256]{2,1,0:T(8,128)(2,1)S(1)}, bf16[4,192,256]{2,1,0:T(8,128)(2,1)S(1)}, f32[288,128]{1,0:T(8,128)S(1)}, f32[288,128]{1,0:T(8,128)S(1)}) custom-call(bf16[2,128,768]{2,1,0:T(8,128)(2,1)S(1)} %get-tuple-element.34.refs_0_, bf16[16,128,256]{2,1,0:T(8,128)(2,1)S(1)} %get-tuple-element.30.refs_2_.refs_1_, ...), custom_call_target="tpu_custom_call" | custom-call | flops 268435456 | bytes 1048576 | tf_op jit(solution)/shard_map/outer/pallas_call | solution.py:480
  13.4 0.1 collective-permute-start.4
  13.5 1.4 %collective-permute-done.4 = f32[288,128]{1,0:T(8,128)S(1)} collective-permute-done((f32[288,128]{1,0:T(8,128)S(1)}, f32[288,128]{1,0:T(8,128)S(1)}, u32[]{:S(2)}, u32[]{:S(2)}) %collective-permute-start.4) | collective-permute-done | bytes 147488 | tf_op jit(solution)/shard_map/ppermute | solution.py:501
  14.8 2.5 %collective-permute-start.7 = (bf16[288,128]{1,0:T(8,128)(2,1)S(1)}, bf16[288,128]{1,0:T(8,128)(2,1)S(1)}, u32[]{:S(2)}, u32[]{:S(2)}) collective-permute-start(bf16[288,128]{1,0:T(8,128)(2,1)S(1)} %add_convert_fusion), channel_id=1, source_target_pairs={{0,20},{1,21},{2,22},{3,23},{4,16},{5,17},{6,18},{7,19},{8,28},{9,... | collective-permute-start | bytes 221192 | tf_op jit(solution)/shard_map/ppermute | solution.py:415
  17.3 0.6 %collective-permute-start.6 = (bf16[288,128]{1,0:T(8,128)(2,1)S(1)}, bf16[288,128]{1,0:T(8,128)(2,1)S(1)}, u32[]{:S(2)}, u32[]{:S(2)}) collective-permute-start(bf16[288,128]{1,0:T(8,128)(2,1)S(1)} %add_convert_fusion), channel_id=1, source_target_pairs={{0,4},{1,5},{2,6},{3,7},{4,0},{5,1},{6,2},{7,3},{8,12},{9,13},{10,... | collective-permute-start | bytes 221192 | tf_op jit(solution)/shard_map/ppermute | solution.py:415
  17.9 0.5 %collective-permute-start.5 = (bf16[288,128]{1,0:T(8,128)(2,1)S(1)}, bf16[288,128]{1,0:T(8,128)(2,1)S(1)}, u32[]{:S(2)}, u32[]{:S(2)}) collective-permute-start(bf16[288,128]{1,0:T(8,128)(2,1)S(1)} %add_convert_fusion), channel_id=1, source_target_pairs={{0,16},{1,17},{2,18},{3,19},{4,20},{5,21},{6,22},{7,23},{8,24},{9,... | collective-permute-start | bytes 221192 | tf_op jit(solution)/shard_map/ppermute | solution.py:415
  18.4 1.5 %out.1 = bf16[1,64,16,256]{3,2,1,0:T(8,128)(2,1)} custom-call(bf16[3,3,64,64]{3,2,1,0:T(8,128)(2,1)S(1)} %get-tuple-element.29.refs_1_.kernel, bf16[14,192,256]{2,1,0:T(8,128)(2,1)S(1)} %get-tuple-element.43.mid, bf16[4,192,256]{2,1,0:T(8,128)(2,1)S(1)} %get-tuple-element.44.ends), custom_call_target="tpu_custom_call" | custom-call | flops 536870912 | bytes 1048576 | tf_op jit(solution)/shard_map/out/pallas_call | solution.py:489
  19.9 0.7 %collective-permute-done.7 = bf16[288,128]{1,0:T(8,128)(2,1)S(1)} collective-permute-done((bf16[288,128]{1,0:T(8,128)(2,1)S(1)}, bf16[288,128]{1,0:T(8,128)(2,1)S(1)}, u32[]{:S(2)}, u32[]{:S(2)}) %collective-permute-start.7) | collective-permute-done | bytes 73760 | tf_op jit(solution)/shard_map/ppermute | solution.py:415
  20.6 1.2 %collective-permute-done.6 = bf16[288,128]{1,0:T(8,128)(2,1)S(1)} collective-permute-done((bf16[288,128]{1,0:T(8,128)(2,1)S(1)}, bf16[288,128]{1,0:T(8,128)(2,1)S(1)}, u32[]{:S(2)}, u32[]{:S(2)}) %collective-permute-start.6) | collective-permute-done | bytes 73760 | tf_op jit(solution)/shard_map/ppermute | solution.py:415
  21.8 0.4 %collective-permute-done.5 = bf16[288,128]{1,0:T(8,128)(2,1)S(1)} collective-permute-done((bf16[288,128]{1,0:T(8,128)(2,1)S(1)}, bf16[288,128]{1,0:T(8,128)(2,1)S(1)}, u32[]{:S(2)}, u32[]{:S(2)}) %collective-permute-start.5) | collective-permute-done | bytes 73760 | tf_op jit(solution)/shard_map/ppermute | solution.py:415
  22.3 6.1 %collective-permute-start.9 = (bf16[288,128]{1,0:T(8,128)(2,1)S(1)}, bf16[288,128]{1,0:T(8,128)(2,1)S(1)}, u32[]{:S(2)}, u32[]{:S(2)}) collective-permute-start(bf16[288,128]{1,0:T(8,128)(2,1)S(1)} %convert_add_fusion.1), channel_id=1, source_target_pairs={{0,2},{1,3},{2,0},{3,1},{4,6},{5,7},{6,4},{7,5},{8,10},{9,11},{10,... | collective-permute-start | bytes 221192 | tf_op jit(solution)/shard_map/ppermute | solution.py:415
  28.4 0.0 collective-permute-start.8
  28.4 1.5 %collective-permute-start.10 = (bf16[288,128]{1,0:T(8,128)(2,1)S(1)}, bf16[288,128]{1,0:T(8,128)(2,1)S(1)}, u32[]{:S(2)}, u32[]{:S(2)}) collective-permute-start(bf16[288,128]{1,0:T(8,128)(2,1)S(1)} %convert_add_fusion.1), channel_id=1, source_target_pairs={{0,3},{1,2},{2,1},{3,0},{4,7},{5,6},{6,5},{7,4},{8,11},{9,10},{10,... | collective-permute-start | bytes 221192 | tf_op jit(solution)/shard_map/ppermute | solution.py:415
  29.9 1.6 %grad_in.1 = bf16[1,64,16,256]{3,2,1,0:T(8,128)(2,1)} custom-call(bf16[3,3,64,64]{3,2,1,0:T(8,128)(2,1)S(1)} %get-tuple-element.28.refs_0_.kernel, bf16[14,192,256]{2,1,0:T(8,128)(2,1)S(1)} %get-tuple-element.37.refs_5_.mid, bf16[4,192,256]{2,1,0:T(8,128)(2,1)S(1)} %get-tuple-element.47.ends), custom_call_target="tpu_custom_call" | custom-call | flops 536870912 | bytes 1048576 | tf_op jit(solution)/shard_map/grad_in/pallas_call | solution.py:489
  31.6 0.0 collective-permute-done.9
  31.6 1.7 %collective-permute-done.8 = bf16[288,128]{1,0:T(8,128)(2,1)S(1)} collective-permute-done((bf16[288,128]{1,0:T(8,128)(2,1)S(1)}, bf16[288,128]{1,0:T(8,128)(2,1)S(1)}, u32[]{:S(2)}, u32[]{:S(2)}) %collective-permute-start.8) | collective-permute-done | bytes 73760 | tf_op jit(solution)/shard_map/ppermute | solution.py:415
  33.3 1.3 %collective-permute-done.10 = bf16[288,128]{1,0:T(8,128)(2,1)S(1)} collective-permute-done((bf16[288,128]{1,0:T(8,128)(2,1)S(1)}, bf16[288,128]{1,0:T(8,128)(2,1)S(1)}, u32[]{:S(2)}, u32[]{:S(2)}) %collective-permute-start.10) | collective-permute-done | bytes 73760 | tf_op jit(solution)/shard_map/ppermute | solution.py:415
  34.7 0.1 collective-permute-start.11
  34.8 1.4 %collective-permute-done.11.other = f32[288,128]{1,0:T(8,128)S(1)} collective-permute-done((f32[288,128]{1,0:T(8,128)S(1)}, f32[288,128]{1,0:T(8,128)S(1)}, u32[]{:S(2)}, u32[]{:S(2)}) %collective-permute-start.11) | collective-permute-done | bytes 147488 | tf_op jit(solution)/shard_map/ppermute | solution.py:514
  36.1 0.9 %finish.1 = (f32[3,3,64,64]{3,2,1,0:T(8,128)}, f32[3,3,64,64]{3,2,1,0:T(8,128)}) custom-call(f32[288,128]{1,0:T(8,128)S(1)} %convert_add_fusion.mine, f32[288,128]{1,0:T(8,128)S(1)} %collective-permute-done.11.other), custom_call_target="tpu_custom_call" | custom-call | bytes 1048576 | tf_op jit(solution)/shard_map/finish/pallas_call | solution.py:516
  (3 shorter events, 0.1 us)
Async XLA Ops:
  2.6 5.3 %collective-permute-start = (bf16[128,128]{1,0:T(8,128)(2,1)S(1)}, bf16[128,128]{1,0:T(8,128)(2,1)S(1)}, u32[]{:S(2)}, u32[]{:S(2)}) collective-permute-start(bf16[128,128]{1,0:T(8,128)(2,1)S(1)} %get-tuple-element.32), channel_id=1, source_target_pairs={{0,1},{1,0},{2,3},{3,2},{4,5},{5,4},{6,7},{7,6},{8,9},{9,8},{10,11... | collective-permute-start | bytes 98312 | tf_op jit(solution)/shard_map/ppermute | solution.py:46
  5.7 2.2 %collective-permute-start.1 = (bf16[128,128]{1,0:T(8,128)(2,1)S(1)}, bf16[128,128]{1,0:T(8,128)(2,1)S(1)}, u32[]{:S(2)}, u32[]{:S(2)}) collective-permute-start(bf16[128,128]{1,0:T(8,128)(2,1)S(1)} %get-tuple-element.33), channel_id=1, source_target_pairs={{1,2},{2,1},{5,6},{6,5},{9,10},{10,9},{13,14},{14,13},{17,18},{18,... | collective-permute-start | bytes 98312 | tf_op jit(solution)/shard_map/ppermute | solution.py:46
  6.4 5.9 %collective-permute-start.2 = (bf16[2,128,256]{2,1,0:T(8,128)(2,1)S(1)}, bf16[2,128,256]{2,1,0:T(8,128)(2,1)S(1)}, u32[]{:S(2)}, u32[]{:S(2)}) collective-permute-start(bf16[2,128,256]{2,1,0:T(8,128)(2,1)S(1)} %get-tuple-element.40), channel_id=1, source_target_pairs={{0,4},{4,0},{1,5},{5,1},{2,6},{6,2},{3,7},{7,3},{8,12},{12,8},{9,1... | collective-permute-start | bytes 393224 | tf_op jit(solution)/shard_map/ppermute | solution.py:46
  8.1 4.1 %collective-permute-start.3 = (bf16[128,128]{1,0:T(8,128)(2,1)S(1)}, bf16[128,128]{1,0:T(8,128)(2,1)S(1)}, u32[]{:S(2)}, u32[]{:S(2)}) collective-permute-start(bf16[128,128]{1,0:T(8,128)(2,1)S(1)} %corner.1), channel_id=1, source_target_pairs={{0,4},{4,0},{1,5},{5,1},{2,6},{6,2},{3,7},{7,3},{8,12},{12,8},{9,1... | collective-permute-start | bytes 98312 | tf_op jit(solution)/shard_map/ppermute | solution.py:46
  13.4 1.4 %collective-permute-start.4 = (f32[288,128]{1,0:T(8,128)S(1)}, f32[288,128]{1,0:T(8,128)S(1)}, u32[]{:S(2)}, u32[]{:S(2)}) collective-permute-start(f32[288,128]{1,0:T(8,128)S(1)} %get-tuple-element.42), channel_id=1, source_target_pairs={{0,8},{8,0},{16,24},{24,16},{1,9},{9,1},{17,25},{25,17},{2,10},{10... | collective-permute-start | bytes 442376 | tf_op jit(solution)/shard_map/ppermute | solution.py:501
  14.8 5.8 %collective-permute-start.7 = (bf16[288,128]{1,0:T(8,128)(2,1)S(1)}, bf16[288,128]{1,0:T(8,128)(2,1)S(1)}, u32[]{:S(2)}, u32[]{:S(2)}) collective-permute-start(bf16[288,128]{1,0:T(8,128)(2,1)S(1)} %add_convert_fusion), channel_id=1, source_target_pairs={{0,20},{1,21},{2,22},{3,23},{4,16},{5,17},{6,18},{7,19},{8,28},{9,... | collective-permute-start | bytes 221192 | tf_op jit(solution)/shard_map/ppermute | solution.py:415
  17.3 4.5 %collective-permute-start.6 = (bf16[288,128]{1,0:T(8,128)(2,1)S(1)}, bf16[288,128]{1,0:T(8,128)(2,1)S(1)}, u32[]{:S(2)}, u32[]{:S(2)}) collective-permute-start(bf16[288,128]{1,0:T(8,128)(2,1)S(1)} %add_convert_fusion), channel_id=1, source_target_pairs={{0,4},{1,5},{2,6},{3,7},{4,0},{5,1},{6,2},{7,3},{8,12},{9,13},{10,... | collective-permute-start | bytes 221192 | tf_op jit(solution)/shard_map/ppermute | solution.py:415
  17.9 4.4 %collective-permute-start.5 = (bf16[288,128]{1,0:T(8,128)(2,1)S(1)}, bf16[288,128]{1,0:T(8,128)(2,1)S(1)}, u32[]{:S(2)}, u32[]{:S(2)}) collective-permute-start(bf16[288,128]{1,0:T(8,128)(2,1)S(1)} %add_convert_fusion), channel_id=1, source_target_pairs={{0,16},{1,17},{2,18},{3,19},{4,20},{5,21},{6,22},{7,23},{8,24},{9,... | collective-permute-start | bytes 221192 | tf_op jit(solution)/shard_map/ppermute | solution.py:415
  22.3 9.3 %collective-permute-start.9 = (bf16[288,128]{1,0:T(8,128)(2,1)S(1)}, bf16[288,128]{1,0:T(8,128)(2,1)S(1)}, u32[]{:S(2)}, u32[]{:S(2)}) collective-permute-start(bf16[288,128]{1,0:T(8,128)(2,1)S(1)} %convert_add_fusion.1), channel_id=1, source_target_pairs={{0,2},{1,3},{2,0},{3,1},{4,6},{5,7},{6,4},{7,5},{8,10},{9,11},{10,... | collective-permute-start | bytes 221192 | tf_op jit(solution)/shard_map/ppermute | solution.py:415
  28.4 4.9 %collective-permute-start.8 = (bf16[288,128]{1,0:T(8,128)(2,1)S(1)}, bf16[288,128]{1,0:T(8,128)(2,1)S(1)}, u32[]{:S(2)}, u32[]{:S(2)}) collective-permute-start(bf16[288,128]{1,0:T(8,128)(2,1)S(1)} %convert_add_fusion.1), channel_id=1, source_target_pairs={{0,1},{1,0},{2,3},{3,2},{4,5},{5,4},{6,7},{7,6},{8,9},{9,8},{10,11... | collective-permute-start | bytes 221192 | tf_op jit(solution)/shard_map/ppermute | solution.py:415
  28.4 6.3 %collective-permute-start.10 = (bf16[288,128]{1,0:T(8,128)(2,1)S(1)}, bf16[288,128]{1,0:T(8,128)(2,1)S(1)}, u32[]{:S(2)}, u32[]{:S(2)}) collective-permute-start(bf16[288,128]{1,0:T(8,128)(2,1)S(1)} %convert_add_fusion.1), channel_id=1, source_target_pairs={{0,3},{1,2},{2,1},{3,0},{4,7},{5,6},{6,5},{7,4},{8,11},{9,10},{10,... | collective-permute-start | bytes 221192 | tf_op jit(solution)/shard_map/ppermute | solution.py:415
  34.7 1.4 %collective-permute-start.11 = (f32[288,128]{1,0:T(8,128)S(1)}, f32[288,128]{1,0:T(8,128)S(1)}, u32[]{:S(2)}, u32[]{:S(2)}) collective-permute-start(f32[288,128]{1,0:T(8,128)S(1)} %convert_add_fusion.mine), channel_id=1, source_target_pairs={{0,8},{8,0},{16,24},{24,16},{1,9},{9,1},{17,25},{25,17},{2,10},{10... | collective-permute-start | bytes 442376 | tf_op jit(solution)/shard_map/ppermute | solution.py:514

commit v2 on v1

--- a/solution.py
+++ b/solution.py
@@ -32,18 +32,23 @@
 
 
 def pairs(size, second):
-    start = 1 if second else 0
-    out = []
-    for i in range(start, size - 1, 2):
-        out += [(i, i + 1), (i + 1, i)]
+    out = list(range(size))
+    for i in range(1 if second else 0, size - 1, 2):
+        out[i], out[i + 1] = i + 1, i
     return out
 
 
 def swap(array, axis, second):
-    perm = pairs(lax.axis_size(axis), second)
-    if not perm:
+    size, n_dp = lax.axis_size(axis), lax.axis_size("dp")
+    partner = pairs(size, second)
+    if partner == list(range(size)):
         return None
-    return lax.ppermute(array, axis, perm)
+    lone = lambda d: d ^ 1 if (d | 1) < n_dp else d
+    perm = []
+    for d in range(n_dp):
+        for i, to in enumerate(partner):
+            perm.append((d * size + i, (lone(d) if to == i else d) * size + to))
+    return lax.ppermute(array, ("dp", axis), perm)
 
 
 def pack_body(
@@ -52,7 +57,7 @@
 ):
     ch, rows, cols = img.shape[1:]
     halves = cols // LANES
-    pitch = wide.shape[2] // ch
+    pitch = wide.shape[2] // (ch + 1)
     col_odd = lax.axis_index("col") % 2 == 1
     row_odd = lax.axis_index("row") % 2 == 1
     lane = lanes_of((ch, LANES))
@@ -105,19 +110,20 @@
         copy.wait()
 
 
-def sides(a, b, odd):
+def sides(a, b, axis):
+    at, size = lax.axis_index(axis), lax.axis_size(axis)
+    b = a if b is None else b
+    odd = at % 2 == 1
     zero = jnp.zeros(a.shape, a.dtype)
-    b = zero if b is None else b
-    return jnp.where(odd, a, b), jnp.where(odd, b, a)
+    before = jnp.where(at > 0, jnp.where(odd, a, b), zero)
+    behind = jnp.where(at < size - 1, jnp.where(odd, b, a), zero)
+    return before, behind
 
 
 def corner_body(rows, strip_a, strip_b, send_a, send_b):
-    col_odd = lax.axis_index("col") % 2 == 1
     row_odd = lax.axis_index("row") % 2 == 1
     lane = lanes_of(strip_a.shape)
-    west, east = sides(
-        strip_a[...].astype(F32), None if strip_b is None else strip_b[...].astype(F32), col_odd
-    )
+    west, east = side_strips(strip_a, strip_b)
     both = jnp.where(lane < 2 * SLOT, west, pltpu.roll(east, 2 * SLOT, 1))
     slot = lane % SLOT
     down = jnp.where(slot < 2, pltpu.roll(both, (-rows) % LANES, 1), 0.0)
@@ -157,7 +163,7 @@
     return sides(
         strip_a[...].astype(F32),
         None if strip_b is None else strip_b[...].astype(F32),
-        lax.axis_index("col") % 2 == 1,
+        "col",
     )
 
 
@@ -275,16 +281,15 @@
     rows, ch2, cols = x16.shape
     ch = ch2 // 2
     has_north, has_south, has_west, has_east = has_neighbours()
+    west, east = side_strips(strip_a, strip_b)
     lane2 = lanes_of((ch2, LANES))
-    west, east = side_strips(strip_a, strip_b)
-    corner = corner_a[...].astype(F32)
-    if corner_b is not None:
-        corner = corner + corner_b[...].astype(F32)
+    above, below = sides(
+        corner_a[...].astype(F32), None if corner_b is None else corner_b[...].astype(F32), "row"
+    )
+    corner = jnp.where(lane2 % SLOT < 2, above, below)
     west = west + jnp.where(lane2 < 2 * SLOT, corner, 0.0)
     east = east + jnp.where(lane2 < 2 * SLOT, pltpu.roll(corner, LANES - 2 * SLOT, 1), 0.0)
-    north, south = sides(
-        row_a[...], None if row_b is None else row_b[...], lax.axis_index("row") % 2 == 1
-    )
+    north, south = sides(row_a[...], None if row_b is None else row_b[...], "row")
     left, right = own[0].astype(F32), own[1].astype(F32)
     first = lanes_of((ch, LANES)) == 0
     last = lanes_of((ch, LANES)) == LANES - 1
@@ -358,7 +363,7 @@
     rows = mid.shape[0] + 2
     ch = kernel.shape[2]
     cols = mid.shape[2]
-    pitch = wide.shape[1] // ch
+    pitch = wide.shape[1] // (ch + 1)
     row_weights(weights, kernel, flip)
     for t in range(rows // 2):
         if t == 0:
@@ -446,7 +451,7 @@
         + [row_pair] * (1 + two_rows),
         [
             pltpu.VMEM((2, ch, rows, cols), BF),
-            pltpu.VMEM((2, halves, ch * pitch, LANES), F32),
+            pltpu.VMEM((2, halves, (ch + 1) * pitch, LANES), F32),
             pltpu.SemaphoreType.DMA((2, PIECES)),
             pltpu.SemaphoreType.DMA((2,)),
         ],
@@ -491,7 +496,7 @@
             [sds(images.shape, BF)],
             [
                 pltpu.VMEM((2 * ch, 12 * ch), BF),
-                pltpu.VMEM((halves, ch * pitch, LANES), F32),
+                pltpu.VMEM((halves, (ch + 1) * pitch, LANES), F32),
             ],
             flops=1 << 29,
             name=name,

time: 37.2 us -> 35.3 us (0.949)
  starting transfers between devices: 18.3 us -> 16 us
  waiting for transfers between devices: 8.11 us -> 8.64 us
    ppermute x6, starting transfers between devices: 11.2 us -> 9.22 us  [exchange(): total = total + lax.ppermute(sent, axes, perm).astype(F32)]
    ppermute x4, waiting for transfers between devices: 0.01 us -> 0.53 us  [swap(): return lax.ppermute(array, ('dp', axis), perm)]
    ppermute x4, starting transfers between devices: 7 us -> 6.61 us  [swap(): return lax.ppermute(array, ('dp', axis), perm)]
  transfers between devices with their start and end apart: 12 -> 12, of which waited for: 7 -> 9; matrix products, arithmetic and copies ran while one was open for 0% -> 0% of each run, Pallas kernels for 16% -> 16%
where the time goes in v2:
time: 35.3 us; the launch traced here: 35.2 us
  starting transfers between devices  16 us (45%)
  Pallas kernels  9.79 us (28%)
  waiting for transfers between devices  8.64 us (24%)
  between operations  0.69 us (2%)
    ppermute x6, starting transfers between devices, exchange(): total = total + lax.ppermute(sent, axes, perm).astype(F32)  9.22 us
    ppermute x4, starting transfers between devices, swap(): return lax.ppermute(array, ('dp', axis), perm)  6.61 us
    ppermute x6, waiting for transfers between devices, exchange(): total = total + lax.ppermute(sent, axes, perm).astype(F32)  5.39 us
    pallas_call x2, Pallas kernels, back(): kernel_call(functools.partial(back_body, flip), [sds(images.shape, BF)],...  3.17 us
    pallas_call x1, Pallas kernels, on_device(): kernel_call(optional(inner_body, [True] * 5 + [two_cols]), [shifted(rows)...  2.42 us
    pallas_call x1, Pallas kernels, on_device(): pack(*[pltpu.with_memory_space_constraint(v, pltpu.HBM) for v in (images,...  1.95 us
    ppermute x1, waiting for transfers between devices, on_device(): total_half = mine + lax.ppermute(other, 'dp', partner)  1.36 us
    ppermute x1, waiting for transfers between devices, on_device(): rest = lax.ppermute(total_half, 'dp', partner)  1.36 us
  transfers between devices with their start and end apart: 12, of which 9 were waited for; matrix products, arithmetic and copies ran while one was open for 0% of the time, Pallas kernels for 16%

profile of v2, /device:TPU:0, one launch (start us, length us, event | category | flops | bytes accessed | tf_op | source)
XLA Modules:
  0.0 35.2 jit_solution(7462323868070977740)
XLA Ops:
  0.6 2.0 %pack.1 = (bf16[16,128,256]{2,1,0:T(8,128)(2,1)S(1)}, bf16[2,128,128]{2,1,0:T(8,128)(2,1)S(1)}, bf16[3,3,64,64]{3,2,1,0:T(8,128)(2,1)S(1)}, bf16[3,3,64,64]{3,2,...) custom-call(bf16[1,64,16,256]{3,2,1,0:T(8,128)(2,1)} %refs_0_.1, ...), custom_call_target="tpu_custom_call" | custom-call | flops 134217728 | bytes 1048576 | tf_op jit(solution)/shard_map/pack/pallas_call | solution.py:462
  2.6 3.1 %collective-permute-start = (bf16[128,128]{1,0:T(8,128)(2,1)S(1)}, bf16[128,128]{1,0:T(8,128)(2,1)S(1)}, u32[]{:S(2)}, u32[]{:S(2)}) collective-permute-start(bf16[128,128]{1,0:T(8,128)(2,1)S(1)} %get-tuple-element.32), channel_id=1, source_target_pairs={{0,1},{1,0},{2,3},{3,2},{8,9},{9,8},{10,11},{11,10},{16,17},{17,16... | collective-permute-start | bytes 98312 | tf_op jit(solution)/shard_map/ppermute | solution.py:51
  5.7 0.0 collective-permute-start.1
  5.7 1.5 %collective-permute-start.2 = (bf16[2,128,256]{2,1,0:T(8,128)(2,1)S(1)}, bf16[2,128,256]{2,1,0:T(8,128)(2,1)S(1)}, u32[]{:S(2)}, u32[]{:S(2)}) collective-permute-start(bf16[2,128,256]{2,1,0:T(8,128)(2,1)S(1)} %get-tuple-element.40), channel_id=1, source_target_pairs={{0,4},{4,0},{8,12},{12,8},{16,20},{20,16},{24,28},{28,24},{1,5},{5... | collective-permute-start | bytes 393224 | tf_op jit(solution)/shard_map/ppermute | solution.py:51
  7.2 0.4 %collective-permute-done.refs_4_.refs_0_.refs_8_ = bf16[128,128]{1,0:T(8,128)(2,1)S(1)} collective-permute-done((bf16[128,128]{1,0:T(8,128)(2,1)S(1)}, bf16[128,128]{1,0:T(8,128)(2,1)S(1)}, u32[]{:S(2)}, u32[]{:S(2)}) %collective-permute-start) | collective-permute-done | bytes 32800 | tf_op jit(solution)/shard_map/ppermute | solution.py:51
  7.6 0.0 collective-permute-done.1.refs_5_.refs_1_.refs_9_
  7.6 0.2 corner.1
  7.8 2.0 %collective-permute-start.3 = (bf16[128,128]{1,0:T(8,128)(2,1)S(1)}, bf16[128,128]{1,0:T(8,128)(2,1)S(1)}, u32[]{:S(2)}, u32[]{:S(2)}) collective-permute-start(bf16[128,128]{1,0:T(8,128)(2,1)S(1)} %corner.1), channel_id=1, source_target_pairs={{0,4},{4,0},{8,12},{12,8},{16,20},{20,16},{24,28},{28,24},{1,5},{5... | collective-permute-start | bytes 98312 | tf_op jit(solution)/shard_map/ppermute | solution.py:51
  9.8 2.4 %inner.1 = (bf16[16,192,256]{2,1,0:T(8,128)(2,1)S(1)}, bf16[16,192,256]{2,1,0:T(8,128)(2,1)S(1)}, bf16[14,192,256]{2,1,0:T(8,128)(2,1)S(1)}, bf16[14,192,256]{2,...) custom-call(bf16[3,3,64,64]{3,2,1,0:T(8,128)(2,1)S(1)} %get-tuple-element.28, ...), custom_call_target="tpu_custom_call" | custom-call | flops 1073741824 | bytes 1048576 | tf_op jit(solution)/shard_map/inner/pallas_call | solution.py:477
  12.2 0.1 collective-permute-done.3.refs_11_
  12.3 0.0 collective-permute-done.2.refs_10_
  12.3 1.2 %outer.1 = (bf16[4,192,256]{2,1,0:T(8,128)(2,1)S(1)}, bf16[4,192,256]{2,1,0:T(8,128)(2,1)S(1)}, f32[288,128]{1,0:T(8,128)S(1)}, f32[288,128]{1,0:T(8,128)S(1)}) custom-call(bf16[2,128,768]{2,1,0:T(8,128)(2,1)S(1)} %get-tuple-element.34.refs_0_, bf16[16,128,256]{2,1,0:T(8,128)(2,1)S(1)} %get-tuple-element.30.refs_2_.refs_1_, ...), custom_call_target="tpu_custom_call" | custom-call | flops 268435456 | bytes 1048576 | tf_op jit(solution)/shard_map/outer/pallas_call | solution.py:485
  13.5 0.1 collective-permute-start.4
  13.6 1.4 %collective-permute-done.4 = f32[288,128]{1,0:T(8,128)S(1)} collective-permute-done((f32[288,128]{1,0:T(8,128)S(1)}, f32[288,128]{1,0:T(8,128)S(1)}, u32[]{:S(2)}, u32[]{:S(2)}) %collective-permute-start.4) | collective-permute-done | bytes 147488 | tf_op jit(solution)/shard_map/ppermute | solution.py:506
  14.9 2.5 %collective-permute-start.7 = (bf16[288,128]{1,0:T(8,128)(2,1)S(1)}, bf16[288,128]{1,0:T(8,128)(2,1)S(1)}, u32[]{:S(2)}, u32[]{:S(2)}) collective-permute-start(bf16[288,128]{1,0:T(8,128)(2,1)S(1)} %add_convert_fusion), channel_id=1, source_target_pairs={{0,20},{1,21},{2,22},{3,23},{4,16},{5,17},{6,18},{7,19},{8,28},{9,... | collective-permute-start | bytes 221192 | tf_op jit(solution)/shard_map/ppermute | solution.py:420
  17.4 0.5 %collective-permute-start.6 = (bf16[288,128]{1,0:T(8,128)(2,1)S(1)}, bf16[288,128]{1,0:T(8,128)(2,1)S(1)}, u32[]{:S(2)}, u32[]{:S(2)}) collective-permute-start(bf16[288,128]{1,0:T(8,128)(2,1)S(1)} %add_convert_fusion), channel_id=1, source_target_pairs={{0,4},{1,5},{2,6},{3,7},{4,0},{5,1},{6,2},{7,3},{8,12},{9,13},{10,... | collective-permute-start | bytes 221192 | tf_op jit(solution)/shard_map/ppermute | solution.py:420
  18.0 0.5 %collective-permute-start.5 = (bf16[288,128]{1,0:T(8,128)(2,1)S(1)}, bf16[288,128]{1,0:T(8,128)(2,1)S(1)}, u32[]{:S(2)}, u32[]{:S(2)}) collective-permute-start(bf16[288,128]{1,0:T(8,128)(2,1)S(1)} %add_convert_fusion), channel_id=1, source_target_pairs={{0,16},{1,17},{2,18},{3,19},{4,20},{5,21},{6,22},{7,23},{8,24},{9,... | collective-permute-start | bytes 221192 | tf_op jit(solution)/shard_map/ppermute | solution.py:420
  18.5 1.5 %out.1 = bf16[1,64,16,256]{3,2,1,0:T(8,128)(2,1)} custom-call(bf16[3,3,64,64]{3,2,1,0:T(8,128)(2,1)S(1)} %get-tuple-element.29.refs_1_.kernel, bf16[14,192,256]{2,1,0:T(8,128)(2,1)S(1)} %get-tuple-element.43.mid, bf16[4,192,256]{2,1,0:T(8,128)(2,1)S(1)} %get-tuple-element.44.ends), custom_call_target="tpu_custom_call" | custom-call | flops 536870912 | bytes 1048576 | tf_op jit(solution)/shard_map/out/pallas_call | solution.py:494
  20.0 0.6 %collective-permute-done.7 = bf16[288,128]{1,0:T(8,128)(2,1)S(1)} collective-permute-done((bf16[288,128]{1,0:T(8,128)(2,1)S(1)}, bf16[288,128]{1,0:T(8,128)(2,1)S(1)}, u32[]{:S(2)}, u32[]{:S(2)}) %collective-permute-start.7) | collective-permute-done | bytes 73760 | tf_op jit(solution)/shard_map/ppermute | solution.py:420
  20.7 1.2 %collective-permute-done.6 = bf16[288,128]{1,0:T(8,128)(2,1)S(1)} collective-permute-done((bf16[288,128]{1,0:T(8,128)(2,1)S(1)}, bf16[288,128]{1,0:T(8,128)(2,1)S(1)}, u32[]{:S(2)}, u32[]{:S(2)}) %collective-permute-start.6) | collective-permute-done | bytes 73760 | tf_op jit(solution)/shard_map/ppermute | solution.py:420
  21.9 0.4 %collective-permute-done.5 = bf16[288,128]{1,0:T(8,128)(2,1)S(1)} collective-permute-done((bf16[288,128]{1,0:T(8,128)(2,1)S(1)}, bf16[288,128]{1,0:T(8,128)(2,1)S(1)}, u32[]{:S(2)}, u32[]{:S(2)}) %collective-permute-start.5) | collective-permute-done | bytes 73760 | tf_op jit(solution)/shard_map/ppermute | solution.py:420
  22.4 4.1 %collective-permute-start.9 = (bf16[288,128]{1,0:T(8,128)(2,1)S(1)}, bf16[288,128]{1,0:T(8,128)(2,1)S(1)}, u32[]{:S(2)}, u32[]{:S(2)}) collective-permute-start(bf16[288,128]{1,0:T(8,128)(2,1)S(1)} %convert_add_fusion.1), channel_id=1, source_target_pairs={{0,2},{1,3},{2,0},{3,1},{4,6},{5,7},{6,4},{7,5},{8,10},{9,11},{10,... | collective-permute-start | bytes 221192 | tf_op jit(solution)/shard_map/ppermute | solution.py:420
  26.5 0.0 collective-permute-start.8
  26.5 1.5 %collective-permute-start.10 = (bf16[288,128]{1,0:T(8,128)(2,1)S(1)}, bf16[288,128]{1,0:T(8,128)(2,1)S(1)}, u32[]{:S(2)}, u32[]{:S(2)}) collective-permute-start(bf16[288,128]{1,0:T(8,128)(2,1)S(1)} %convert_add_fusion.1), channel_id=1, source_target_pairs={{0,3},{1,2},{2,1},{3,0},{4,7},{5,6},{6,5},{7,4},{8,11},{9,10},{10,... | collective-permute-start | bytes 221192 | tf_op jit(solution)/shard_map/ppermute | solution.py:420
  28.1 1.6 %grad_in.1 = bf16[1,64,16,256]{3,2,1,0:T(8,128)(2,1)} custom-call(bf16[3,3,64,64]{3,2,1,0:T(8,128)(2,1)S(1)} %get-tuple-element.28.refs_0_.kernel, bf16[14,192,256]{2,1,0:T(8,128)(2,1)S(1)} %get-tuple-element.37.refs_5_.mid, bf16[4,192,256]{2,1,0:T(8,128)(2,1)S(1)} %get-tuple-element.47.ends), custom_call_target="tpu_custom_call" | custom-call | flops 536870912 | bytes 1048576 | tf_op jit(solution)/shard_map/grad_in/pallas_call | solution.py:494
  29.7 0.0 collective-permute-done.9
  29.7 1.7 %collective-permute-done.8 = bf16[288,128]{1,0:T(8,128)(2,1)S(1)} collective-permute-done((bf16[288,128]{1,0:T(8,128)(2,1)S(1)}, bf16[288,128]{1,0:T(8,128)(2,1)S(1)}, u32[]{:S(2)}, u32[]{:S(2)}) %collective-permute-start.8) | collective-permute-done | bytes 73760 | tf_op jit(solution)/shard_map/ppermute | solution.py:420
  31.4 1.3 %collective-permute-done.10 = bf16[288,128]{1,0:T(8,128)(2,1)S(1)} collective-permute-done((bf16[288,128]{1,0:T(8,128)(2,1)S(1)}, bf16[288,128]{1,0:T(8,128)(2,1)S(1)}, u32[]{:S(2)}, u32[]{:S(2)}) %collective-permute-start.10) | collective-permute-done | bytes 73760 | tf_op jit(solution)/shard_map/ppermute | solution.py:420
  32.8 0.1 collective-permute-start.11
  32.9 1.4 %collective-permute-done.11.other = f32[288,128]{1,0:T(8,128)S(1)} collective-permute-done((f32[288,128]{1,0:T(8,128)S(1)}, f32[288,128]{1,0:T(8,128)S(1)}, u32[]{:S(2)}, u32[]{:S(2)}) %collective-permute-start.11) | collective-permute-done | bytes 147488 | tf_op jit(solution)/shard_map/ppermute | solution.py:519
  34.3 0.9 %finish.1 = (f32[3,3,64,64]{3,2,1,0:T(8,128)}, f32[3,3,64,64]{3,2,1,0:T(8,128)}) custom-call(f32[288,128]{1,0:T(8,128)S(1)} %convert_add_fusion.mine, f32[288,128]{1,0:T(8,128)S(1)} %collective-permute-done.11.other), custom_call_target="tpu_custom_call" | custom-call | bytes 1048576 | tf_op jit(solution)/shard_map/finish/pallas_call | solution.py:521
  (3 shorter events, 0.1 us)
Async XLA Ops:
  2.6 5.0 %collective-permute-start = (bf16[128,128]{1,0:T(8,128)(2,1)S(1)}, bf16[128,128]{1,0:T(8,128)(2,1)S(1)}, u32[]{:S(2)}, u32[]{:S(2)}) collective-permute-start(bf16[128,128]{1,0:T(8,128)(2,1)S(1)} %get-tuple-element.32), channel_id=1, source_target_pairs={{0,1},{1,0},{2,3},{3,2},{8,9},{9,8},{10,11},{11,10},{16,17},{17,16... | collective-permute-start | bytes 98312 | tf_op jit(solution)/shard_map/ppermute | solution.py:51
  5.7 1.9 %collective-permute-start.1 = (bf16[128,128]{1,0:T(8,128)(2,1)S(1)}, bf16[128,128]{1,0:T(8,128)(2,1)S(1)}, u32[]{:S(2)}, u32[]{:S(2)}) collective-permute-start(bf16[128,128]{1,0:T(8,128)(2,1)S(1)} %get-tuple-element.33), channel_id=1, source_target_pairs={{0,8},{1,2},{2,1},{3,11},{8,0},{9,10},{10,9},{11,3},{16,24},{17,18... | collective-permute-start | bytes 98312 | tf_op jit(solution)/shard_map/ppermute | solution.py:51
  5.7 6.6 %collective-permute-start.2 = (bf16[2,128,256]{2,1,0:T(8,128)(2,1)S(1)}, bf16[2,128,256]{2,1,0:T(8,128)(2,1)S(1)}, u32[]{:S(2)}, u32[]{:S(2)}) collective-permute-start(bf16[2,128,256]{2,1,0:T(8,128)(2,1)S(1)} %get-tuple-element.40), channel_id=1, source_target_pairs={{0,4},{4,0},{8,12},{12,8},{16,20},{20,16},{24,28},{28,24},{1,5},{5... | collective-permute-start | bytes 393224 | tf_op jit(solution)/shard_map/ppermute | solution.py:51
  7.8 4.5 %collective-permute-start.3 = (bf16[128,128]{1,0:T(8,128)(2,1)S(1)}, bf16[128,128]{1,0:T(8,128)(2,1)S(1)}, u32[]{:S(2)}, u32[]{:S(2)}) collective-permute-start(bf16[128,128]{1,0:T(8,128)(2,1)S(1)} %corner.1), channel_id=1, source_target_pairs={{0,4},{4,0},{8,12},{12,8},{16,20},{20,16},{24,28},{28,24},{1,5},{5... | collective-permute-start | bytes 98312 | tf_op jit(solution)/shard_map/ppermute | solution.py:51
  13.5 1.4 %collective-permute-start.4 = (f32[288,128]{1,0:T(8,128)S(1)}, f32[288,128]{1,0:T(8,128)S(1)}, u32[]{:S(2)}, u32[]{:S(2)}) collective-permute-start(f32[288,128]{1,0:T(8,128)S(1)} %get-tuple-element.42), channel_id=1, source_target_pairs={{0,8},{8,0},{16,24},{24,16},{1,9},{9,1},{17,25},{25,17},{2,10},{10... | collective-permute-start | bytes 442376 | tf_op jit(solution)/shard_map/ppermute | solution.py:506
  14.9 5.7 %collective-permute-start.7 = (bf16[288,128]{1,0:T(8,128)(2,1)S(1)}, bf16[288,128]{1,0:T(8,128)(2,1)S(1)}, u32[]{:S(2)}, u32[]{:S(2)}) collective-permute-start(bf16[288,128]{1,0:T(8,128)(2,1)S(1)} %add_convert_fusion), channel_id=1, source_target_pairs={{0,20},{1,21},{2,22},{3,23},{4,16},{5,17},{6,18},{7,19},{8,28},{9,... | collective-permute-start | bytes 221192 | tf_op jit(solution)/shard_map/ppermute | solution.py:420
  17.4 4.4 %collective-permute-start.6 = (bf16[288,128]{1,0:T(8,128)(2,1)S(1)}, bf16[288,128]{1,0:T(8,128)(2,1)S(1)}, u32[]{:S(2)}, u32[]{:S(2)}) collective-permute-start(bf16[288,128]{1,0:T(8,128)(2,1)S(1)} %add_convert_fusion), channel_id=1, source_target_pairs={{0,4},{1,5},{2,6},{3,7},{4,0},{5,1},{6,2},{7,3},{8,12},{9,13},{10,... | collective-permute-start | bytes 221192 | tf_op jit(solution)/shard_map/ppermute | solution.py:420
  18.0 4.4 %collective-permute-start.5 = (bf16[288,128]{1,0:T(8,128)(2,1)S(1)}, bf16[288,128]{1,0:T(8,128)(2,1)S(1)}, u32[]{:S(2)}, u32[]{:S(2)}) collective-permute-start(bf16[288,128]{1,0:T(8,128)(2,1)S(1)} %add_convert_fusion), channel_id=1, source_target_pairs={{0,16},{1,17},{2,18},{3,19},{4,20},{5,21},{6,22},{7,23},{8,24},{9,... | collective-permute-start | bytes 221192 | tf_op jit(solution)/shard_map/ppermute | solution.py:420
  22.4 7.3 %collective-permute-start.9 = (bf16[288,128]{1,0:T(8,128)(2,1)S(1)}, bf16[288,128]{1,0:T(8,128)(2,1)S(1)}, u32[]{:S(2)}, u32[]{:S(2)}) collective-permute-start(bf16[288,128]{1,0:T(8,128)(2,1)S(1)} %convert_add_fusion.1), channel_id=1, source_target_pairs={{0,2},{1,3},{2,0},{3,1},{4,6},{5,7},{6,4},{7,5},{8,10},{9,11},{10,... | collective-permute-start | bytes 221192 | tf_op jit(solution)/shard_map/ppermute | solution.py:420
  26.5 4.9 %collective-permute-start.8 = (bf16[288,128]{1,0:T(8,128)(2,1)S(1)}, bf16[288,128]{1,0:T(8,128)(2,1)S(1)}, u32[]{:S(2)}, u32[]{:S(2)}) collective-permute-start(bf16[288,128]{1,0:T(8,128)(2,1)S(1)} %convert_add_fusion.1), channel_id=1, source_target_pairs={{0,1},{1,0},{2,3},{3,2},{4,5},{5,4},{6,7},{7,6},{8,9},{9,8},{10,11... | collective-permute-start | bytes 221192 | tf_op jit(solution)/shard_map/ppermute | solution.py:420
  26.5 6.3 %collective-permute-start.10 = (bf16[288,128]{1,0:T(8,128)(2,1)S(1)}, bf16[288,128]{1,0:T(8,128)(2,1)S(1)}, u32[]{:S(2)}, u32[]{:S(2)}) collective-permute-start(bf16[288,128]{1,0:T(8,128)(2,1)S(1)} %convert_add_fusion.1), channel_id=1, source_target_pairs={{0,3},{1,2},{2,1},{3,0},{4,7},{5,6},{6,5},{7,4},{8,11},{9,10},{10,... | collective-permute-start | bytes 221192 | tf_op jit(solution)/shard_map/ppermute | solution.py:420
  32.8 1.4 %collective-permute-start.11 = (f32[288,128]{1,0:T(8,128)S(1)}, f32[288,128]{1,0:T(8,128)S(1)}, u32[]{:S(2)}, u32[]{:S(2)}) collective-permute-start(f32[288,128]{1,0:T(8,128)S(1)} %convert_add_fusion.mine), channel_id=1, source_target_pairs={{0,8},{8,0},{16,24},{24,16},{1,9},{9,1},{17,25},{25,17},{2,10},{10... | collective-permute-start | bytes 442376 | tf_op jit(solution)/shard_map/ppermute | solution.py:519

commit v3 on v2

--- a/solution.py
+++ b/solution.py
@@ -11,7 +11,7 @@
 BF = jnp.bfloat16
 F32 = jnp.float32
 LANES = 128
-SLOT = 32
+SLOT = LANES // 2
 PIECES = 2
 
 
@@ -92,13 +92,12 @@
             for h in range(rows):
                 v = wide[which, half, pl.ds(h, ch, stride=pitch), :]
                 x16[h, base : base + ch, half * LANES : (half + 1) * LANES] = v.astype(BF)
-                for j in range(2):
-                    at = j * SLOT + h + 2
-                    if half == 0:
-                        left = jnp.where(lane == at, pltpu.roll(v, (at - j) % LANES, 1), left)
-                    if half == halves - 1:
-                        src = LANES - 2 + j
-                        right = jnp.where(lane == at, pltpu.roll(v, (at - src) % LANES, 1), right)
+                at = 2 * (h + 2)
+                here = (lane >= at) & (lane < at + 2)
+                if half == 0:
+                    left = jnp.where(here, pltpu.roll(v, at, 1), left)
+                if half == halves - 1:
+                    right = jnp.where(here, pltpu.roll(v, (at + 2) % LANES, 1), right)
         own[0, base : base + ch, :] = left.astype(BF)
         own[1, base : base + ch, :] = right.astype(BF)
         send_a[base : base + ch, :] = jnp.where(col_odd, left, right).astype(BF)
@@ -124,10 +123,11 @@
     row_odd = lax.axis_index("row") % 2 == 1
     lane = lanes_of(strip_a.shape)
     west, east = side_strips(strip_a, strip_b)
-    both = jnp.where(lane < 2 * SLOT, west, pltpu.roll(east, 2 * SLOT, 1))
+    both = jnp.where(lane < SLOT, west, pltpu.roll(east, SLOT, 1))
     slot = lane % SLOT
-    down = jnp.where(slot < 2, pltpu.roll(both, (-rows) % LANES, 1), 0.0)
-    up = jnp.where((slot >= rows + 2) & (slot < rows + 4), pltpu.roll(both, rows, 1), 0.0)
+    down = jnp.where(slot < 4, pltpu.roll(both, (-2 * rows) % LANES, 1), 0.0)
+    far = (slot >= 2 * (rows + 2)) & (slot < 2 * (rows + 4))
+    up = jnp.where(far, pltpu.roll(both, (2 * rows) % LANES, 1), 0.0)
     send_a[...] = jnp.where(row_odd, up, down).astype(BF)
     if send_b is not None:
         send_b[...] = jnp.where(row_odd, down, up).astype(BF)
@@ -167,25 +167,29 @@
     )
 
 
-def edge_of(before, behind, lane_before, lane_behind):
-    near = lanes_of(before.shape) < LANES // 2
-    return jnp.where(
-        near,
-        pltpu.roll(before, (-lane_before) % LANES, 1),
-        pltpu.roll(behind, (LANES - 1 - lane_behind) % LANES, 1),
-    )
+def even_lanes(shape):
+    return lanes_of(shape) % 2 == 0
+
+
+def edge_of(strips, h):
+    return pltpu.roll(strips, (-2 * (h + 2) - 1) % LANES, 1)
 
 
 def border(weights, west, east, left, right):
-    e0 = lanes_of(west.shape) < SLOT
-    b0 = jnp.where(e0, west, right)
-    b1 = jnp.where(e0, pltpu.roll(west, LANES - SLOT, 1), pltpu.roll(east, SLOT, 1))
-    b2 = jnp.where(e0, left, east)
+    even = even_lanes(west.shape)
+    b0 = jnp.where(even, west, right)
+    b1 = jnp.where(even, pltpu.roll(west, LANES - 1, 1), pltpu.roll(east, 1, 1))
+    b2 = jnp.where(even, left, east)
     taps = []
     for a in range(3):
-        taps += [pltpu.roll(b, (1 - a) % LANES, 1) if a != 1 else b for b in (b0, b1, b2)]
+        taps += [pltpu.roll(b, (2 - 2 * a) % LANES, 1) if a != 1 else b for b in (b0, b1, b2)]
     stack = jnp.concatenate(taps, 0).astype(BF)
     return jnp.dot(weights, stack, preferred_element_type=F32)
+
+
+def crossed(strips):
+    v = strips.astype(BF)
+    return jnp.where(even_lanes(v.shape), pltpu.roll(v, LANES - 1, 1), pltpu.roll(v, 1, 1))
 
 
 def activation(hidden, act_grad):
@@ -228,22 +232,22 @@
     left, right = own[0].astype(F32), own[1].astype(F32)
     first = lanes_of((ch, LANES)) == 0
     last = lanes_of((ch, LANES)) == LANES - 1
-    west_b, east_b = west.astype(BF), east.astype(BF)
+    near = jnp.where(even_lanes(west.shape), east, west).astype(BF)
     for h in range(rows):
-        edge = edge_of(west_b, east_b, SLOT + h + 2, h + 2)
+        edge = edge_of(near, h)
         for which, dst in enumerate((xi, xc)):
             s = slice(which * ch, (which + 1) * ch)
             put_shifted(dst, h, halves_of(x16[h, s]), edge[s], first, last)
     lane = lanes_of((ch, LANES))
     _, _, has_west, has_east = has_neighbours()
-    keep = jnp.where(lane < SLOT, has_west, has_east) > 0.0
+    keep = jnp.where(lane % 2 == 0, has_west, has_east) > 0.0
     sides_of = lambda s: (west[s], east[s], left[s], right[s])
     act_e, hid_e = activation(
         border(wf[0, :ch, : 9 * ch], *sides_of(slice(0, ch))),
         border(wf[1, :ch, : 9 * ch], *sides_of(slice(ch, ch2))),
     )
-    act_e = jnp.where(keep, act_e, 0.0).astype(BF)
-    hid_e = jnp.where(keep, hid_e, 0.0).astype(BF)
+    act_e = crossed(jnp.where(keep, act_e, 0.0))
+    hid_e = crossed(jnp.where(keep, hid_e, 0.0))
     zero_row = jnp.zeros((ch, cols), BF)
     for t in range((rows - 2) // 2):
         at = 2 * t
@@ -258,7 +262,7 @@
                 h = at + p + 1
                 put_shifted(
                     dst, at + p, halves_of(values[p * ch : (p + 1) * ch].astype(BF)),
-                    edge_of(e, e, h + 2, SLOT + h + 2), first, last,
+                    edge_of(e, h), first, last,
                 )
     g1 = jnp.zeros((3 * ch, 3 * ch), F32)
     for r in range(rows):
@@ -286,37 +290,35 @@
     above, below = sides(
         corner_a[...].astype(F32), None if corner_b is None else corner_b[...].astype(F32), "row"
     )
-    corner = jnp.where(lane2 % SLOT < 2, above, below)
-    west = west + jnp.where(lane2 < 2 * SLOT, corner, 0.0)
-    east = east + jnp.where(lane2 < 2 * SLOT, pltpu.roll(corner, LANES - 2 * SLOT, 1), 0.0)
+    corner = jnp.where(lane2 % SLOT < 4, above, below)
+    west = west + jnp.where(lane2 < SLOT, corner, 0.0)
+    east = east + jnp.where(lane2 < SLOT, pltpu.roll(corner, SLOT, 1), 0.0)
     north, south = sides(row_a[...], None if row_b is None else row_b[...], "row")
     left, right = own[0].astype(F32), own[1].astype(F32)
     first = lanes_of((ch, LANES)) == 0
     last = lanes_of((ch, LANES)) == LANES - 1
-    west_b, east_b = west.astype(BF), east.astype(BF)
+    near = jnp.where(even_lanes(west.shape), east, west).astype(BF)
     for k in range(4):
         slot = k if k < 2 else rows + k
         row = (north if k < 2 else south)[k % 2]
         lo, hi = row[:, :LANES].astype(F32), row[:, cols - LANES :].astype(F32)
-        left = jnp.where(lane2 == slot, pltpu.roll(lo, slot, 1), left)
-        right = jnp.where(
-            lane2 == SLOT + slot, pltpu.roll(hi, (SLOT + slot - LANES + 1) % LANES, 1), right
-        )
-        edge = edge_of(west_b, east_b, SLOT + slot, slot)
+        left = jnp.where(lane2 == 2 * slot, pltpu.roll(lo, 2 * slot, 1), left)
+        right = jnp.where(lane2 == 2 * slot + 1, pltpu.roll(hi, (2 * slot + 2) % LANES, 1), right)
+        edge = edge_of(near, slot - 2)
         for which in range(2):
             s = slice(which * ch, (which + 1) * ch)
             put_shifted(xo.at[which], k, halves_of(row[s]), edge[s], first, last)
     lane = lanes_of((ch, LANES))
-    slots = lane % SLOT
-    keep = jnp.where(lane < SLOT, has_west, has_east)
+    slots = lane // 2
+    keep = jnp.where(lane % 2 == 0, has_west, has_east)
     keep = keep * jnp.where(slots == 1, has_north, 1.0) * jnp.where(slots == rows + 2, has_south, 1.0)
     sides_of = lambda s: (west[s], east[s], left[s], right[s])
     act_e, hid_e = activation(
         border(wf[0, :ch, : 9 * ch], *sides_of(slice(0, ch))),
         border(wf[1, :ch, : 9 * ch], *sides_of(slice(ch, ch2))),
     )
-    act_e = jnp.where(keep > 0.0, act_e, 0.0).astype(BF)
-    hid_e = jnp.where(keep > 0.0, hid_e, 0.0).astype(BF)
+    act_e = crossed(jnp.where(keep > 0.0, act_e, 0.0))
+    hid_e = crossed(jnp.where(keep > 0.0, hid_e, 0.0))
     for t in range(2):
         stacks = []
         for which, mid in enumerate((xi, xc)):
@@ -338,7 +340,7 @@
                 if at == 3:
                     v = jnp.where(has_south > 0.0, v, 0.0)
                 put_shifted(
-                    dst, at, halves_of(v.astype(BF)), edge_of(e, e, h + 2, SLOT + h + 2), first, last
+                    dst, at, halves_of(v.astype(BF)), edge_of(e, h), first, last
                 )
     zero_row = jnp.zeros((ch, cols), BF)
     g1, g2 = g1_in[...], g2_in[...]

time: 35.3 us -> 35.1 us (level)
  no operation moved by 1% of the time
where the time goes in v3:
time: 35.1 us; the launch traced here: 35 us
  starting transfers between devices  15.9 us (45%)
  Pallas kernels  9.56 us (27%)
  waiting for transfers between devices  8.68 us (25%)
  between operations  0.69 us (2%)
    ppermute x6, starting transfers between devices, exchange(): total = total + lax.ppermute(sent, axes, perm).astype(F32)  9.2 us
    ppermute x4, starting transfers between devices, swap(): return lax.ppermute(array, ('dp', axis), perm)  6.61 us
    ppermute x6, waiting for transfers between devices, exchange(): total = total + lax.ppermute(sent, axes, perm).astype(F32)  5.39 us
    pallas_call x2, Pallas kernels, back(): kernel_call(functools.partial(back_body, flip), [sds(images.shape, BF)],...  3.17 us
    pallas_call x1, Pallas kernels, on_device(): kernel_call(optional(inner_body, [True] * 5 + [two_cols]), [shifted(rows)...  2.37 us
    pallas_call x1, Pallas kernels, on_device(): pack(*[pltpu.with_memory_space_constraint(v, pltpu.HBM) for v in (images,...  1.76 us
    ppermute x1, waiting for transfers between devices, on_device(): total_half = mine + lax.ppermute(other, 'dp', partner)  1.36 us
    ppermute x1, waiting for transfers between devices, on_device(): rest = lax.ppermute(total_half, 'dp', partner)  1.36 us
  transfers between devices with their start and end apart: 12, of which 9 were waited for; matrix products, arithmetic and copies ran while one was open for 0% of the time, Pallas kernels for 16%

profile of v3, /device:TPU:0, one launch (start us, length us, event | category | flops | bytes accessed | tf_op | source)
XLA Modules:
  0.0 35.0 jit_solution(741127415221871474)
XLA Ops:
  0.6 1.8 %pack.1 = (bf16[16,128,256]{2,1,0:T(8,128)(2,1)S(1)}, bf16[2,128,128]{2,1,0:T(8,128)(2,1)S(1)}, bf16[3,3,64,64]{3,2,1,0:T(8,128)(2,1)S(1)}, bf16[3,3,64,64]{3,2,...) custom-call(bf16[1,64,16,256]{3,2,1,0:T(8,128)(2,1)} %refs_0_.1, ...), custom_call_target="tpu_custom_call" | custom-call | flops 134217728 | bytes 1048576 | tf_op jit(solution)/shard_map/pack/pallas_call | solution.py:464
  2.4 3.1 %collective-permute-start = (bf16[128,128]{1,0:T(8,128)(2,1)S(1)}, bf16[128,128]{1,0:T(8,128)(2,1)S(1)}, u32[]{:S(2)}, u32[]{:S(2)}) collective-permute-start(bf16[128,128]{1,0:T(8,128)(2,1)S(1)} %get-tuple-element.32), channel_id=1, source_target_pairs={{0,1},{1,0},{2,3},{3,2},{8,9},{9,8},{10,11},{11,10},{16,17},{17,16... | collective-permute-start | bytes 98312 | tf_op jit(solution)/shard_map/ppermute | solution.py:51
  5.5 0.0 collective-permute-start.1
  5.5 1.5 %collective-permute-start.2 = (bf16[2,128,256]{2,1,0:T(8,128)(2,1)S(1)}, bf16[2,128,256]{2,1,0:T(8,128)(2,1)S(1)}, u32[]{:S(2)}, u32[]{:S(2)}) collective-permute-start(bf16[2,128,256]{2,1,0:T(8,128)(2,1)S(1)} %get-tuple-element.40), channel_id=1, source_target_pairs={{0,4},{4,0},{8,12},{12,8},{16,20},{20,16},{24,28},{28,24},{1,5},{5... | collective-permute-start | bytes 393224 | tf_op jit(solution)/shard_map/ppermute | solution.py:51
  7.0 0.4 %collective-permute-done.refs_4_.refs_0_.refs_8_ = bf16[128,128]{1,0:T(8,128)(2,1)S(1)} collective-permute-done((bf16[128,128]{1,0:T(8,128)(2,1)S(1)}, bf16[128,128]{1,0:T(8,128)(2,1)S(1)}, u32[]{:S(2)}, u32[]{:S(2)}) %collective-permute-start) | collective-permute-done | bytes 32800 | tf_op jit(solution)/shard_map/ppermute | solution.py:51
  7.4 0.0 collective-permute-done.1.refs_5_.refs_1_.refs_9_
  7.4 0.2 corner.1
  7.6 2.0 %collective-permute-start.3 = (bf16[128,128]{1,0:T(8,128)(2,1)S(1)}, bf16[128,128]{1,0:T(8,128)(2,1)S(1)}, u32[]{:S(2)}, u32[]{:S(2)}) collective-permute-start(bf16[128,128]{1,0:T(8,128)(2,1)S(1)} %corner.1), channel_id=1, source_target_pairs={{0,4},{4,0},{8,12},{12,8},{16,20},{20,16},{24,28},{28,24},{1,5},{5... | collective-permute-start | bytes 98312 | tf_op jit(solution)/shard_map/ppermute | solution.py:51
  9.6 2.4 %inner.1 = (bf16[16,192,256]{2,1,0:T(8,128)(2,1)S(1)}, bf16[16,192,256]{2,1,0:T(8,128)(2,1)S(1)}, bf16[14,192,256]{2,1,0:T(8,128)(2,1)S(1)}, bf16[14,192,256]{2,...) custom-call(bf16[3,3,64,64]{3,2,1,0:T(8,128)(2,1)S(1)} %get-tuple-element.28, ...), custom_call_target="tpu_custom_call" | custom-call | flops 1073741824 | bytes 1048576 | tf_op jit(solution)/shard_map/inner/pallas_call | solution.py:479
  12.0 0.2 collective-permute-done.3.refs_11_
  12.1 0.0 collective-permute-done.2.refs_10_
  12.1 1.2 %outer.1 = (bf16[4,192,256]{2,1,0:T(8,128)(2,1)S(1)}, bf16[4,192,256]{2,1,0:T(8,128)(2,1)S(1)}, f32[288,128]{1,0:T(8,128)S(1)}, f32[288,128]{1,0:T(8,128)S(1)}) custom-call(bf16[2,128,768]{2,1,0:T(8,128)(2,1)S(1)} %get-tuple-element.34.refs_0_, bf16[16,128,256]{2,1,0:T(8,128)(2,1)S(1)} %get-tuple-element.30.refs_2_.refs_1_, ...), custom_call_target="tpu_custom_call" | custom-call | flops 268435456 | bytes 1048576 | tf_op jit(solution)/shard_map/outer/pallas_call | solution.py:487
  13.3 0.1 collective-permute-start.4
  13.4 1.4 %collective-permute-done.4 = f32[288,128]{1,0:T(8,128)S(1)} collective-permute-done((f32[288,128]{1,0:T(8,128)S(1)}, f32[288,128]{1,0:T(8,128)S(1)}, u32[]{:S(2)}, u32[]{:S(2)}) %collective-permute-start.4) | collective-permute-done | bytes 147488 | tf_op jit(solution)/shard_map/ppermute | solution.py:508
  14.7 2.5 %collective-permute-start.7 = (bf16[288,128]{1,0:T(8,128)(2,1)S(1)}, bf16[288,128]{1,0:T(8,128)(2,1)S(1)}, u32[]{:S(2)}, u32[]{:S(2)}) collective-permute-start(bf16[288,128]{1,0:T(8,128)(2,1)S(1)} %add_convert_fusion), channel_id=1, source_target_pairs={{0,20},{1,21},{2,22},{3,23},{4,16},{5,17},{6,18},{7,19},{8,28},{9,... | collective-permute-start | bytes 221192 | tf_op jit(solution)/shard_map/ppermute | solution.py:422
  17.3 0.5 %collective-permute-start.6 = (bf16[288,128]{1,0:T(8,128)(2,1)S(1)}, bf16[288,128]{1,0:T(8,128)(2,1)S(1)}, u32[]{:S(2)}, u32[]{:S(2)}) collective-permute-start(bf16[288,128]{1,0:T(8,128)(2,1)S(1)} %add_convert_fusion), channel_id=1, source_target_pairs={{0,4},{1,5},{2,6},{3,7},{4,0},{5,1},{6,2},{7,3},{8,12},{9,13},{10,... | collective-permute-start | bytes 221192 | tf_op jit(solution)/shard_map/ppermute | solution.py:422
  17.8 0.5 %collective-permute-start.5 = (bf16[288,128]{1,0:T(8,128)(2,1)S(1)}, bf16[288,128]{1,0:T(8,128)(2,1)S(1)}, u32[]{:S(2)}, u32[]{:S(2)}) collective-permute-start(bf16[288,128]{1,0:T(8,128)(2,1)S(1)} %add_convert_fusion), channel_id=1, source_target_pairs={{0,16},{1,17},{2,18},{3,19},{4,20},{5,21},{6,22},{7,23},{8,24},{9,... | collective-permute-start | bytes 221192 | tf_op jit(solution)/shard_map/ppermute | solution.py:422
  18.3 1.5 %out.1 = bf16[1,64,16,256]{3,2,1,0:T(8,128)(2,1)} custom-call(bf16[3,3,64,64]{3,2,1,0:T(8,128)(2,1)S(1)} %get-tuple-element.29.refs_1_.kernel, bf16[14,192,256]{2,1,0:T(8,128)(2,1)S(1)} %get-tuple-element.43.mid, bf16[4,192,256]{2,1,0:T(8,128)(2,1)S(1)} %get-tuple-element.44.ends), custom_call_target="tpu_custom_call" | custom-call | flops 536870912 | bytes 1048576 | tf_op jit(solution)/shard_map/out/pallas_call | solution.py:496
  19.8 0.6 %collective-permute-done.7 = bf16[288,128]{1,0:T(8,128)(2,1)S(1)} collective-permute-done((bf16[288,128]{1,0:T(8,128)(2,1)S(1)}, bf16[288,128]{1,0:T(8,128)(2,1)S(1)}, u32[]{:S(2)}, u32[]{:S(2)}) %collective-permute-start.7) | collective-permute-done | bytes 73760 | tf_op jit(solution)/shard_map/ppermute | solution.py:422
  20.5 1.2 %collective-permute-done.6 = bf16[288,128]{1,0:T(8,128)(2,1)S(1)} collective-permute-done((bf16[288,128]{1,0:T(8,128)(2,1)S(1)}, bf16[288,128]{1,0:T(8,128)(2,1)S(1)}, u32[]{:S(2)}, u32[]{:S(2)}) %collective-permute-start.6) | collective-permute-done | bytes 73760 | tf_op jit(solution)/shard_map/ppermute | solution.py:422
  21.7 0.4 %collective-permute-done.5 = bf16[288,128]{1,0:T(8,128)(2,1)S(1)} collective-permute-done((bf16[288,128]{1,0:T(8,128)(2,1)S(1)}, bf16[288,128]{1,0:T(8,128)(2,1)S(1)}, u32[]{:S(2)}, u32[]{:S(2)}) %collective-permute-start.5) | collective-permute-done | bytes 73760 | tf_op jit(solution)/shard_map/ppermute | solution.py:422
  22.2 4.1 %collective-permute-start.9 = (bf16[288,128]{1,0:T(8,128)(2,1)S(1)}, bf16[288,128]{1,0:T(8,128)(2,1)S(1)}, u32[]{:S(2)}, u32[]{:S(2)}) collective-permute-start(bf16[288,128]{1,0:T(8,128)(2,1)S(1)} %convert_add_fusion.1), channel_id=1, source_target_pairs={{0,2},{1,3},{2,0},{3,1},{4,6},{5,7},{6,4},{7,5},{8,10},{9,11},{10,... | collective-permute-start | bytes 221192 | tf_op jit(solution)/shard_map/ppermute | solution.py:422
  26.3 0.0 collective-permute-start.8
  26.3 1.5 %collective-permute-start.10 = (bf16[288,128]{1,0:T(8,128)(2,1)S(1)}, bf16[288,128]{1,0:T(8,128)(2,1)S(1)}, u32[]{:S(2)}, u32[]{:S(2)}) collective-permute-start(bf16[288,128]{1,0:T(8,128)(2,1)S(1)} %convert_add_fusion.1), channel_id=1, source_target_pairs={{0,3},{1,2},{2,1},{3,0},{4,7},{5,6},{6,5},{7,4},{8,11},{9,10},{10,... | collective-permute-start | bytes 221192 | tf_op jit(solution)/shard_map/ppermute | solution.py:422
  27.8 1.6 %grad_in.1 = bf16[1,64,16,256]{3,2,1,0:T(8,128)(2,1)} custom-call(bf16[3,3,64,64]{3,2,1,0:T(8,128)(2,1)S(1)} %get-tuple-element.28.refs_0_.kernel, bf16[14,192,256]{2,1,0:T(8,128)(2,1)S(1)} %get-tuple-element.37.refs_5_.mid, bf16[4,192,256]{2,1,0:T(8,128)(2,1)S(1)} %get-tuple-element.47.ends), custom_call_target="tpu_custom_call" | custom-call | flops 536870912 | bytes 1048576 | tf_op jit(solution)/shard_map/grad_in/pallas_call | solution.py:496
  29.5 0.0 collective-permute-done.9
  29.5 1.7 %collective-permute-done.8 = bf16[288,128]{1,0:T(8,128)(2,1)S(1)} collective-permute-done((bf16[288,128]{1,0:T(8,128)(2,1)S(1)}, bf16[288,128]{1,0:T(8,128)(2,1)S(1)}, u32[]{:S(2)}, u32[]{:S(2)}) %collective-permute-start.8) | collective-permute-done | bytes 73760 | tf_op jit(solution)/shard_map/ppermute | solution.py:422
  31.2 1.4 %collective-permute-done.10 = bf16[288,128]{1,0:T(8,128)(2,1)S(1)} collective-permute-done((bf16[288,128]{1,0:T(8,128)(2,1)S(1)}, bf16[288,128]{1,0:T(8,128)(2,1)S(1)}, u32[]{:S(2)}, u32[]{:S(2)}) %collective-permute-start.10) | collective-permute-done | bytes 73760 | tf_op jit(solution)/shard_map/ppermute | solution.py:422
  32.6 0.1 collective-permute-start.11
  32.7 1.4 %collective-permute-done.11.other = f32[288,128]{1,0:T(8,128)S(1)} collective-permute-done((f32[288,128]{1,0:T(8,128)S(1)}, f32[288,128]{1,0:T(8,128)S(1)}, u32[]{:S(2)}, u32[]{:S(2)}) %collective-permute-start.11) | collective-permute-done | bytes 147488 | tf_op jit(solution)/shard_map/ppermute | solution.py:521
  34.0 0.9 %finish.1 = (f32[3,3,64,64]{3,2,1,0:T(8,128)}, f32[3,3,64,64]{3,2,1,0:T(8,128)}) custom-call(f32[288,128]{1,0:T(8,128)S(1)} %convert_add_fusion.mine, f32[288,128]{1,0:T(8,128)S(1)} %collective-permute-done.11.other), custom_call_target="tpu_custom_call" | custom-call | bytes 1048576 | tf_op jit(solution)/shard_map/finish/pallas_call | solution.py:523
  (3 shorter events, 0.1 us)
Async XLA Ops:
  2.4 5.0 %collective-permute-start = (bf16[128,128]{1,0:T(8,128)(2,1)S(1)}, bf16[128,128]{1,0:T(8,128)(2,1)S(1)}, u32[]{:S(2)}, u32[]{:S(2)}) collective-permute-start(bf16[128,128]{1,0:T(8,128)(2,1)S(1)} %get-tuple-element.32), channel_id=1, source_target_pairs={{0,1},{1,0},{2,3},{3,2},{8,9},{9,8},{10,11},{11,10},{16,17},{17,16... | collective-permute-start | bytes 98312 | tf_op jit(solution)/shard_map/ppermute | solution.py:51
  5.5 1.9 %collective-permute-start.1 = (bf16[128,128]{1,0:T(8,128)(2,1)S(1)}, bf16[128,128]{1,0:T(8,128)(2,1)S(1)}, u32[]{:S(2)}, u32[]{:S(2)}) collective-permute-start(bf16[128,128]{1,0:T(8,128)(2,1)S(1)} %get-tuple-element.33), channel_id=1, source_target_pairs={{0,8},{1,2},{2,1},{3,11},{8,0},{9,10},{10,9},{11,3},{16,24},{17,18... | collective-permute-start | bytes 98312 | tf_op jit(solution)/shard_map/ppermute | solution.py:51
  5.5 6.6 %collective-permute-start.2 = (bf16[2,128,256]{2,1,0:T(8,128)(2,1)S(1)}, bf16[2,128,256]{2,1,0:T(8,128)(2,1)S(1)}, u32[]{:S(2)}, u32[]{:S(2)}) collective-permute-start(bf16[2,128,256]{2,1,0:T(8,128)(2,1)S(1)} %get-tuple-element.40), channel_id=1, source_target_pairs={{0,4},{4,0},{8,12},{12,8},{16,20},{20,16},{24,28},{28,24},{1,5},{5... | collective-permute-start | bytes 393224 | tf_op jit(solution)/shard_map/ppermute | solution.py:51
  7.6 4.5 %collective-permute-start.3 = (bf16[128,128]{1,0:T(8,128)(2,1)S(1)}, bf16[128,128]{1,0:T(8,128)(2,1)S(1)}, u32[]{:S(2)}, u32[]{:S(2)}) collective-permute-start(bf16[128,128]{1,0:T(8,128)(2,1)S(1)} %corner.1), channel_id=1, source_target_pairs={{0,4},{4,0},{8,12},{12,8},{16,20},{20,16},{24,28},{28,24},{1,5},{5... | collective-permute-start | bytes 98312 | tf_op jit(solution)/shard_map/ppermute | solution.py:51
  13.3 1.4 %collective-permute-start.4 = (f32[288,128]{1,0:T(8,128)S(1)}, f32[288,128]{1,0:T(8,128)S(1)}, u32[]{:S(2)}, u32[]{:S(2)}) collective-permute-start(f32[288,128]{1,0:T(8,128)S(1)} %get-tuple-element.42), channel_id=1, source_target_pairs={{0,8},{8,0},{16,24},{24,16},{1,9},{9,1},{17,25},{25,17},{2,10},{10... | collective-permute-start | bytes 442376 | tf_op jit(solution)/shard_map/ppermute | solution.py:508
  14.7 5.7 %collective-permute-start.7 = (bf16[288,128]{1,0:T(8,128)(2,1)S(1)}, bf16[288,128]{1,0:T(8,128)(2,1)S(1)}, u32[]{:S(2)}, u32[]{:S(2)}) collective-permute-start(bf16[288,128]{1,0:T(8,128)(2,1)S(1)} %add_convert_fusion), channel_id=1, source_target_pairs={{0,20},{1,21},{2,22},{3,23},{4,16},{5,17},{6,18},{7,19},{8,28},{9,... | collective-permute-start | bytes 221192 | tf_op jit(solution)/shard_map/ppermute | solution.py:422
  17.3 4.4 %collective-permute-start.6 = (bf16[288,128]{1,0:T(8,128)(2,1)S(1)}, bf16[288,128]{1,0:T(8,128)(2,1)S(1)}, u32[]{:S(2)}, u32[]{:S(2)}) collective-permute-start(bf16[288,128]{1,0:T(8,128)(2,1)S(1)} %add_convert_fusion), channel_id=1, source_target_pairs={{0,4},{1,5},{2,6},{3,7},{4,0},{5,1},{6,2},{7,3},{8,12},{9,13},{10,... | collective-permute-start | bytes 221192 | tf_op jit(solution)/shard_map/ppermute | solution.py:422
  17.8 4.4 %collective-permute-start.5 = (bf16[288,128]{1,0:T(8,128)(2,1)S(1)}, bf16[288,128]{1,0:T(8,128)(2,1)S(1)}, u32[]{:S(2)}, u32[]{:S(2)}) collective-permute-start(bf16[288,128]{1,0:T(8,128)(2,1)S(1)} %add_convert_fusion), channel_id=1, source_target_pairs={{0,16},{1,17},{2,18},{3,19},{4,20},{5,21},{6,22},{7,23},{8,24},{9,... | collective-permute-start | bytes 221192 | tf_op jit(solution)/shard_map/ppermute | solution.py:422
  22.2 7.3 %collective-permute-start.9 = (bf16[288,128]{1,0:T(8,128)(2,1)S(1)}, bf16[288,128]{1,0:T(8,128)(2,1)S(1)}, u32[]{:S(2)}, u32[]{:S(2)}) collective-permute-start(bf16[288,128]{1,0:T(8,128)(2,1)S(1)} %convert_add_fusion.1), channel_id=1, source_target_pairs={{0,2},{1,3},{2,0},{3,1},{4,6},{5,7},{6,4},{7,5},{8,10},{9,11},{10,... | collective-permute-start | bytes 221192 | tf_op jit(solution)/shard_map/ppermute | solution.py:422
  26.3 4.9 %collective-permute-start.8 = (bf16[288,128]{1,0:T(8,128)(2,1)S(1)}, bf16[288,128]{1,0:T(8,128)(2,1)S(1)}, u32[]{:S(2)}, u32[]{:S(2)}) collective-permute-start(bf16[288,128]{1,0:T(8,128)(2,1)S(1)} %convert_add_fusion.1), channel_id=1, source_target_pairs={{0,1},{1,0},{2,3},{3,2},{4,5},{5,4},{6,7},{7,6},{8,9},{9,8},{10,11... | collective-permute-start | bytes 221192 | tf_op jit(solution)/shard_map/ppermute | solution.py:422
  26.3 6.3 %collective-permute-start.10 = (bf16[288,128]{1,0:T(8,128)(2,1)S(1)}, bf16[288,128]{1,0:T(8,128)(2,1)S(1)}, u32[]{:S(2)}, u32[]{:S(2)}) collective-permute-start(bf16[288,128]{1,0:T(8,128)(2,1)S(1)} %convert_add_fusion.1), channel_id=1, source_target_pairs={{0,3},{1,2},{2,1},{3,0},{4,7},{5,6},{6,5},{7,4},{8,11},{9,10},{10,... | collective-permute-start | bytes 221192 | tf_op jit(solution)/shard_map/ppermute | solution.py:422
  32.6 1.4 %collective-permute-start.11 = (f32[288,128]{1,0:T(8,128)S(1)}, f32[288,128]{1,0:T(8,128)S(1)}, u32[]{:S(2)}, u32[]{:S(2)}) collective-permute-start(f32[288,128]{1,0:T(8,128)S(1)} %convert_add_fusion.mine), channel_id=1, source_target_pairs={{0,8},{8,0},{16,24},{24,16},{1,9},{9,1},{17,25},{25,17},{2,10},{10... | collective-permute-start | bytes 442376 | tf_op jit(solution)/shard_map/ppermute | solution.py:521

commit v4 on v3

--- a/solution.py
+++ b/solution.py
@@ -242,12 +242,8 @@
     _, _, has_west, has_east = has_neighbours()
     keep = jnp.where(lane % 2 == 0, has_west, has_east) > 0.0
     sides_of = lambda s: (west[s], east[s], left[s], right[s])
-    act_e, hid_e = activation(
-        border(wf[0, :ch, : 9 * ch], *sides_of(slice(0, ch))),
-        border(wf[1, :ch, : 9 * ch], *sides_of(slice(ch, ch2))),
-    )
-    act_e = crossed(jnp.where(keep, act_e, 0.0))
-    hid_e = crossed(jnp.where(keep, hid_e, 0.0))
+    hidden_e = border(wf[0, :ch, : 9 * ch], *sides_of(slice(0, ch)))
+    act_e = crossed(jnp.where(keep, activation(hidden_e, hidden_e)[0], 0.0))
     zero_row = jnp.zeros((ch, cols), BF)
     for t in range((rows - 2) // 2):
         at = 2 * t
@@ -257,17 +253,17 @@
         act_grad = jnp.dot(
             wf[1], xc[at : at + 4].reshape(12 * ch, cols), preferred_element_type=F32
         )
-        for values, dst, e in zip(activation(hidden, act_grad), (acts, hids), (act_e, hid_e)):
-            for p in range(2):
-                h = at + p + 1
-                put_shifted(
-                    dst, at + p, halves_of(values[p * ch : (p + 1) * ch].astype(BF)),
-                    edge_of(e, h), first, last,
-                )
+        act, hid = [v.astype(BF) for v in activation(hidden, act_grad)]
+        for p in range(2):
+            own_rows = slice(p * ch, (p + 1) * ch)
+            hids[at + p] = hid[own_rows]
+            put_shifted(
+                acts, at + p, halves_of(act[own_rows]), edge_of(act_e, at + p + 1), first, last
+            )
     g1 = jnp.zeros((3 * ch, 3 * ch), F32)
     for r in range(rows):
         lhs = [
-            hids[h - 1, ch : 2 * ch] if 1 <= h <= rows - 2 else zero_row for h in range(r - 1, r + 2)
+            hids[h - 1] if 1 <= h <= rows - 2 else zero_row for h in range(r - 1, r + 2)
         ]
         g1 = add_grads(g1, lhs, xi[r])
     g1_out[...] = g1
@@ -280,7 +276,7 @@
 def outer_body(
     wf, x16, own, xi, xc, hids, g1_in, g2_in,
     strip_a, strip_b, row_a, row_b, corner_a, corner_b,
-    acts_o, hids_o, mine, other, xo, grads,
+    acts_o, hids_o, hid_edge, mine, other, xo,
 ):
     rows, ch2, cols = x16.shape
     ch = ch2 // 2
@@ -318,7 +314,7 @@
         border(wf[1, :ch, : 9 * ch], *sides_of(slice(ch, ch2))),
     )
     act_e = crossed(jnp.where(keep > 0.0, act_e, 0.0))
-    hid_e = crossed(jnp.where(keep > 0.0, hid_e, 0.0))
+    hid_edge[...] = crossed(jnp.where(keep > 0.0, hid_e, 0.0))
     for t in range(2):
         stacks = []
         for which, mid in enumerate((xi, xc)):
@@ -330,7 +326,7 @@
             stacks.append(jnp.concatenate(stack, 0))
         hidden = jnp.dot(wf[0], stacks[0], preferred_element_type=F32)
         act_grad = jnp.dot(wf[1], stacks[1], preferred_element_type=F32)
-        for values, dst, e in zip(activation(hidden, act_grad), (acts_o, hids_o), (act_e, hid_e)):
+        for values, dst in zip(activation(hidden, act_grad), (acts_o, hids_o)):
             for p in range(2):
                 at = 2 * t + p
                 h = at - 1 if t == 0 else rows - 3 + at
@@ -339,36 +335,46 @@
                     v = jnp.where(has_north > 0.0, v, 0.0)
                 if at == 3:
                     v = jnp.where(has_south > 0.0, v, 0.0)
-                put_shifted(
-                    dst, at, halves_of(v.astype(BF)), edge_of(e, h), first, last
-                )
+                if dst is hids_o:
+                    dst[at] = v.astype(BF)
+                else:
+                    put_shifted(dst, at, halves_of(v.astype(BF)), edge_of(act_e, h), first, last)
     zero_row = jnp.zeros((ch, cols), BF)
     g1, g2 = g1_in[...], g2_in[...]
     for k, r in ((0, -1), (1, 0), (2, rows - 1), (3, rows)):
         lhs = [x16[h, ch:] if 0 <= h < rows else zero_row for h in range(r - 1, r + 2)]
         g2 = add_grads(g2, lhs, acts_o[k])
-    for h, row in ((0, hids_o[1, ch : 2 * ch]), (rows - 1, hids_o[2, ch : 2 * ch])):
+    for h, row in ((0, hids_o[1]), (rows - 1, hids_o[2])):
         for r in range(h - 1, h + 2):
             rhs = xi[r] if 0 <= r < rows else xo[0, 1 if r < 0 else 2]
             lhs = [row if h == r - 1 + k else zero_row for k in range(3)]
             g1 = add_grads(g1, lhs, rhs)
-    grads[0 : 3 * ch, :] = g1[:, : 2 * ch]
-    grads[3 * ch : 6 * ch, :] = g2[:, : 2 * ch]
-    grads[6 * ch : 9 * ch, :] = jnp.concatenate([g1[:, 2 * ch :], g2[:, 2 * ch :]], 1)
     count = mine.shape[0]
-    core = lax.axis_index("dp") % 2
-    mine[...] = grads[pl.ds(core * count, count), :]
-    other[...] = grads[pl.ds((1 - core) * count, count), :]
-
-
-def back_body(flip, kernel, mid, ends, out, weights, wide):
+    cut = count - 3 * ch
+    low = jnp.concatenate([g1[:, : 2 * ch], g2[:cut, : 2 * ch]], 0)
+    tail = jnp.concatenate([g1[:, 2 * ch :], g2[:, 2 * ch :]], 1)
+    high = jnp.concatenate([g2[cut:, : 2 * ch], tail], 0)
+    leads = lax.axis_index("dp") % 2 == 0
+    mine[...] = jnp.where(leads, low, high)
+    other[...] = jnp.where(leads, high, low)
+
+
+def back_body(flip, kernel, mid, ends, edge, out, weights, wide, shifted):
     rows = mid.shape[0] + 2
     ch = kernel.shape[2]
     cols = mid.shape[2]
     pitch = wide.shape[1] // (ch + 1)
     row_weights(weights, kernel, flip)
+    if edge is not None:
+        first = lanes_of((ch, LANES)) == 0
+        last = lanes_of((ch, LANES)) == LANES - 1
+        for at in range(rows + 2):
+            row = ends[at] if at < 2 else mid[at - 2] if at < rows else ends[at - rows + 2]
+            put_shifted(shifted, at, halves_of(row), edge_of(edge[...], at - 1), first, last)
     for t in range(rows // 2):
-        if t == 0:
+        if edge is not None:
+            stack = shifted[2 * t : 2 * t + 4]
+        elif t == 0:
             stack = jnp.concatenate([ends[0:2], mid[0:2]], 0)
         elif t == rows // 2 - 1:
             stack = jnp.concatenate([mid[rows - 4 : rows - 2], ends[2:4]], 0)
@@ -478,31 +484,30 @@
     sums = sds((3 * ch, 3 * ch), F32)
     xi, xc, acts, hids, g1, g2, wf = kernel_call(
         optional(inner_body, [True] * 5 + [two_cols]),
-        [shifted(rows), shifted(rows), shifted(rows - 2), shifted(rows - 2), sums, sums]
+        [shifted(rows), shifted(rows), shifted(rows - 2), sds((rows - 2, ch, cols), BF), sums, sums]
         + [sds((2, 2 * ch, 12 * ch), BF)],
         flops=1 << 30,
         name="inner",
     )(taps1, taps2, x16, own, *strips)
     half = sds((9 * ch // 2, LANES), F32)
-    acts_o, hids_o, mine, other = kernel_call(
+    acts_o, hids_o, hid_edge, mine, other = kernel_call(
         optional(outer_body, [True] * 8 + [True, two_cols] + [True, two_rows] * 2),
-        [shifted(4), shifted(4), half, half],
-        [pltpu.VMEM((2, 4, 3 * ch, cols), BF), pltpu.VMEM((9 * ch, LANES), F32)],
+        [shifted(4), sds((4, ch, cols), BF), sds((ch, LANES), BF), half, half],
+        [pltpu.VMEM((2, 4, 3 * ch, cols), BF)],
         flops=1 << 28,
         name="outer",
     )(wf, x16, own, xi, xc, hids, g1, g2, *strips, *got_rows, *corners)
 
-    def back(kernel, mid, ends, flip, name):
-        return kernel_call(
-            functools.partial(back_body, flip),
-            [sds(images.shape, BF)],
-            [
-                pltpu.VMEM((2 * ch, 12 * ch), BF),
-                pltpu.VMEM((halves, (ch + 1) * pitch, LANES), F32),
-            ],
-            flops=1 << 29,
-            name=name,
-        )(kernel, mid, ends)[0]
+    def back(kernel, mid, ends, flip, name, edge=()):
+        scratch = [
+            pltpu.VMEM((2 * ch, 12 * ch), BF),
+            pltpu.VMEM((halves, (ch + 1) * pitch, LANES), F32),
+            pltpu.VMEM((rows + 2, 3 * ch, cols), BF),
+        ]
+        body = optional(functools.partial(back_body, flip), [True] * 3 + [bool(edge)])
+        return kernel_call(body, [sds(images.shape, BF)], scratch, flops=1 << 29, name=name)(
+            kernel, mid, ends, *edge
+        )[0]
 
     partner = [(i, i ^ 1) for i in range(n_dp)]
     total_half = mine + lax.ppermute(other, "dp", partner)
@@ -510,7 +515,7 @@
     steps += [(1, 1 << k) for k in range(n_row.bit_length() - 1)]
     steps += [(2, 1 << k) for k in range(n_col.bit_length() - 1)]
     out = back(taps2, acts, acts_o, False, "out")
-    grad_in = back(taps1, hids, hids_o, True, "grad_in")
+    grad_in = back(taps1, hids, hids_o, True, "grad_in", (hid_edge,))
     stages = [steps[k : k + 2] for k in range(0, len(steps), 2)]
     for k, stage in enumerate(stages):
         total_half = exchange(total_half, stage)

time: 35.1 us -> 35.1 us (level)
  transfers between devices with their start and end apart: 12 -> 12, of which waited for: 9 -> 9; matrix products, arithmetic and copies ran while one was open for 0% -> 0% of each run, Pallas kernels for 16% -> 17%
where the time goes in v4:
time: 35.1 us; the launch traced here: 34.9 us
  starting transfers between devices  16 us (46%)
  Pallas kernels  9.69 us (28%)
  waiting for transfers between devices  8.49 us (24%)
  between operations  0.69 us (2%)
    ppermute x6, starting transfers between devices, exchange(): total = total + lax.ppermute(sent, axes, perm).astype(F32)  9.2 us
    ppermute x4, starting transfers between devices, swap(): return lax.ppermute(array, ('dp', axis), perm)  6.61 us
    ppermute x6, waiting for transfers between devices, exchange(): total = total + lax.ppermute(sent, axes, perm).astype(F32)  5.23 us
    pallas_call x2, Pallas kernels, back(): kernel_call(body, [sds(images.shape, BF)], scratch, flops=1 << 29, name=n...  3.34 us
    pallas_call x1, Pallas kernels, on_device(): kernel_call(optional(inner_body, [True] * 5 + [two_cols]), [shifted(rows)...  2.39 us
    pallas_call x1, Pallas kernels, on_device(): pack(*[pltpu.with_memory_space_constraint(v, pltpu.HBM) for v in (images,...  1.76 us
    ppermute x1, waiting for transfers between devices, on_device(): total_half = mine + lax.ppermute(other, 'dp', partner)  1.36 us
    ppermute x1, waiting for transfers between devices, on_device(): rest = lax.ppermute(total_half, 'dp', partner)  1.36 us
  transfers between devices with their start and end apart: 12, of which 9 were waited for; matrix products, arithmetic and copies ran while one was open for 0% of the time, Pallas kernels for 17%

profile of v4, /device:TPU:0, one launch (start us, length us, event | category | flops | bytes accessed | tf_op | source)
XLA Modules:
  0.0 34.9 jit_solution(7379169372466933953)
XLA Ops:
  0.6 1.8 %pack.1 = (bf16[16,128,256]{2,1,0:T(8,128)(2,1)S(1)}, bf16[2,128,128]{2,1,0:T(8,128)(2,1)S(1)}, bf16[3,3,64,64]{3,2,1,0:T(8,128)(2,1)S(1)}, bf16[3,3,64,64]{3,2,...) custom-call(bf16[1,64,16,256]{3,2,1,0:T(8,128)(2,1)} %refs_0_.1, ...), custom_call_target="tpu_custom_call" | custom-call | flops 134217728 | bytes 1048576 | tf_op jit(solution)/shard_map/pack/pallas_call | solution.py:470
  2.4 3.1 %collective-permute-start = (bf16[128,128]{1,0:T(8,128)(2,1)S(1)}, bf16[128,128]{1,0:T(8,128)(2,1)S(1)}, u32[]{:S(2)}, u32[]{:S(2)}) collective-permute-start(bf16[128,128]{1,0:T(8,128)(2,1)S(1)} %get-tuple-element.33), channel_id=1, source_target_pairs={{0,1},{1,0},{2,3},{3,2},{8,9},{9,8},{10,11},{11,10},{16,17},{17,16... | collective-permute-start | bytes 98312 | tf_op jit(solution)/shard_map/ppermute | solution.py:51
  5.5 0.0 collective-permute-start.1
  5.5 1.5 %collective-permute-start.2 = (bf16[2,128,256]{2,1,0:T(8,128)(2,1)S(1)}, bf16[2,128,256]{2,1,0:T(8,128)(2,1)S(1)}, u32[]{:S(2)}, u32[]{:S(2)}) collective-permute-start(bf16[2,128,256]{2,1,0:T(8,128)(2,1)S(1)} %get-tuple-element.41), channel_id=1, source_target_pairs={{0,4},{4,0},{8,12},{12,8},{16,20},{20,16},{24,28},{28,24},{1,5},{5... | collective-permute-start | bytes 393224 | tf_op jit(solution)/shard_map/ppermute | solution.py:51
  7.0 0.4 %collective-permute-done.refs_4_.refs_0_.refs_8_ = bf16[128,128]{1,0:T(8,128)(2,1)S(1)} collective-permute-done((bf16[128,128]{1,0:T(8,128)(2,1)S(1)}, bf16[128,128]{1,0:T(8,128)(2,1)S(1)}, u32[]{:S(2)}, u32[]{:S(2)}) %collective-permute-start) | collective-permute-done | bytes 32800 | tf_op jit(solution)/shard_map/ppermute | solution.py:51
  7.4 0.0 collective-permute-done.1.refs_5_.refs_1_.refs_9_
  7.4 0.2 corner.1
  7.6 2.0 %collective-permute-start.3 = (bf16[128,128]{1,0:T(8,128)(2,1)S(1)}, bf16[128,128]{1,0:T(8,128)(2,1)S(1)}, u32[]{:S(2)}, u32[]{:S(2)}) collective-permute-start(bf16[128,128]{1,0:T(8,128)(2,1)S(1)} %corner.1), channel_id=1, source_target_pairs={{0,4},{4,0},{8,12},{12,8},{16,20},{20,16},{24,28},{28,24},{1,5},{5... | collective-permute-start | bytes 98312 | tf_op jit(solution)/shard_map/ppermute | solution.py:51
  9.6 2.4 %inner.1 = (bf16[16,192,256]{2,1,0:T(8,128)(2,1)S(1)}, bf16[16,192,256]{2,1,0:T(8,128)(2,1)S(1)}, bf16[14,192,256]{2,1,0:T(8,128)(2,1)S(1)}, bf16[14,64,256]{2,1...) custom-call(bf16[3,3,64,64]{3,2,1,0:T(8,128)(2,1)S(1)} %get-tuple-element.29., ...), custom_call_target="tpu_custom_call" | custom-call | flops 1073741824 | bytes 1048576 | tf_op jit(solution)/shard_map/inner/pallas_call | solution.py:485
  12.0 0.1 collective-permute-done.3.refs_11_
  12.1 0.0 collective-permute-done.2.refs_10_
  12.1 1.1 %outer.1 = (bf16[4,192,256]{2,1,0:T(8,128)(2,1)S(1)}, bf16[4,64,256]{2,1,0:T(8,128)(2,1)S(1)}, bf16[64,128]{1,0:T(8,128)(2,1)S(1)}, f32[288,128]{1,0:T(8,128)S(1)}, f32[288,128]{1,0:T(8,128)S(1)}) custom-call(bf16[2,128,768]{2,1,0:T(8,128)(2,1)S(1)} %get-tuple-element.35.refs_0_, bf16[16,128,256]{2,1,0:T(8,128)(2,1)S(1)} %get-tuple-element.31.refs_2_.refs_1_, ...), custom_call_target="tpu_custom_call" | custom-call | flops 268435456 | bytes 1048576 | tf_op jit(solution)/shard_map/outer/pallas_call | solution.py:493
  13.2 0.1 collective-permute-start.4
  13.3 1.4 %collective-permute-done.4 = f32[288,128]{1,0:T(8,128)S(1)} collective-permute-done((f32[288,128]{1,0:T(8,128)S(1)}, f32[288,128]{1,0:T(8,128)S(1)}, u32[]{:S(2)}, u32[]{:S(2)}) %collective-permute-start.4) | collective-permute-done | bytes 147488 | tf_op jit(solution)/shard_map/ppermute | solution.py:513
  14.7 2.5 %collective-permute-start.7 = (bf16[288,128]{1,0:T(8,128)(2,1)S(1)}, bf16[288,128]{1,0:T(8,128)(2,1)S(1)}, u32[]{:S(2)}, u32[]{:S(2)}) collective-permute-start(bf16[288,128]{1,0:T(8,128)(2,1)S(1)} %add_convert_fusion), channel_id=1, source_target_pairs={{0,20},{1,21},{2,22},{3,23},{4,16},{5,17},{6,18},{7,19},{8,28},{9,... | collective-permute-start | bytes 221192 | tf_op jit(solution)/shard_map/ppermute | solution.py:428
  17.2 0.5 %collective-permute-start.6 = (bf16[288,128]{1,0:T(8,128)(2,1)S(1)}, bf16[288,128]{1,0:T(8,128)(2,1)S(1)}, u32[]{:S(2)}, u32[]{:S(2)}) collective-permute-start(bf16[288,128]{1,0:T(8,128)(2,1)S(1)} %add_convert_fusion), channel_id=1, source_target_pairs={{0,4},{1,5},{2,6},{3,7},{4,0},{5,1},{6,2},{7,3},{8,12},{9,13},{10,... | collective-permute-start | bytes 221192 | tf_op jit(solution)/shard_map/ppermute | solution.py:428
  17.7 0.5 %collective-permute-start.5 = (bf16[288,128]{1,0:T(8,128)(2,1)S(1)}, bf16[288,128]{1,0:T(8,128)(2,1)S(1)}, u32[]{:S(2)}, u32[]{:S(2)}) collective-permute-start(bf16[288,128]{1,0:T(8,128)(2,1)S(1)} %add_convert_fusion), channel_id=1, source_target_pairs={{0,16},{1,17},{2,18},{3,19},{4,20},{5,21},{6,22},{7,23},{8,24},{9,... | collective-permute-start | bytes 221192 | tf_op jit(solution)/shard_map/ppermute | solution.py:428
  18.3 1.5 %out.1 = bf16[1,64,16,256]{3,2,1,0:T(8,128)(2,1)} custom-call(bf16[3,3,64,64]{3,2,1,0:T(8,128)(2,1)S(1)} %get-tuple-element.30.refs_1_.refs_0_, bf16[14,192,256]{2,1,0:T(8,128)(2,1)S(1)} %get-tuple-element.44.refs_1_, bf16[4,192,256]{2,1,0:T(8,128)(2,1)S(1)} %get-tuple-element.45.refs_2_), custom_call_target="tpu_custom_call" | custom-call | flops 536870912 | bytes 1048576 | tf_op jit(solution)/shard_map/out/pallas_call | solution.py:508
  19.8 0.6 %collective-permute-done.7 = bf16[288,128]{1,0:T(8,128)(2,1)S(1)} collective-permute-done((bf16[288,128]{1,0:T(8,128)(2,1)S(1)}, bf16[288,128]{1,0:T(8,128)(2,1)S(1)}, u32[]{:S(2)}, u32[]{:S(2)}) %collective-permute-start.7) | collective-permute-done | bytes 73760 | tf_op jit(solution)/shard_map/ppermute | solution.py:428
  20.4 1.2 %collective-permute-done.6 = bf16[288,128]{1,0:T(8,128)(2,1)S(1)} collective-permute-done((bf16[288,128]{1,0:T(8,128)(2,1)S(1)}, bf16[288,128]{1,0:T(8,128)(2,1)S(1)}, u32[]{:S(2)}, u32[]{:S(2)}) %collective-permute-start.6) | collective-permute-done | bytes 73760 | tf_op jit(solution)/shard_map/ppermute | solution.py:428
  21.7 0.4 %collective-permute-done.5 = bf16[288,128]{1,0:T(8,128)(2,1)S(1)} collective-permute-done((bf16[288,128]{1,0:T(8,128)(2,1)S(1)}, bf16[288,128]{1,0:T(8,128)(2,1)S(1)}, u32[]{:S(2)}, u32[]{:S(2)}) %collective-permute-start.5) | collective-permute-done | bytes 73760 | tf_op jit(solution)/shard_map/ppermute | solution.py:428
  22.1 4.1 %collective-permute-start.9 = (bf16[288,128]{1,0:T(8,128)(2,1)S(1)}, bf16[288,128]{1,0:T(8,128)(2,1)S(1)}, u32[]{:S(2)}, u32[]{:S(2)}) collective-permute-start(bf16[288,128]{1,0:T(8,128)(2,1)S(1)} %convert_add_fusion.1), channel_id=1, source_target_pairs={{0,2},{1,3},{2,0},{3,1},{4,6},{5,7},{6,4},{7,5},{8,10},{9,11},{10,... | collective-permute-start | bytes 221192 | tf_op jit(solution)/shard_map/ppermute | solution.py:428
  26.3 0.0 collective-permute-start.8
  26.3 1.5 %collective-permute-start.10 = (bf16[288,128]{1,0:T(8,128)(2,1)S(1)}, bf16[288,128]{1,0:T(8,128)(2,1)S(1)}, u32[]{:S(2)}, u32[]{:S(2)}) collective-permute-start(bf16[288,128]{1,0:T(8,128)(2,1)S(1)} %convert_add_fusion.1), channel_id=1, source_target_pairs={{0,3},{1,2},{2,1},{3,0},{4,7},{5,6},{6,5},{7,4},{8,11},{9,10},{10,... | collective-permute-start | bytes 221192 | tf_op jit(solution)/shard_map/ppermute | solution.py:428
  27.8 1.8 %grad_in.1 = bf16[1,64,16,256]{3,2,1,0:T(8,128)(2,1)} custom-call(bf16[3,3,64,64]{3,2,1,0:T(8,128)(2,1)S(1)} %get-tuple-element.29.refs_0_, bf16[14,64,256]{2,1,0:T(8,128)(2,1)S(1)} %get-tuple-element.38.refs_5_.refs_1_, bf16[4,64,256]{2,1,0:T(8,128)(2,1)S(1)} %get-tuple-element.48.refs_2_, bf16[64,128]{1,0:T(8,128)(2,1)S(1)} %get-tuple-element.49.refs_3_), custom_call_target="tpu_custom_call" | custom-call | flops 536870912 | bytes 1048576 | tf_op jit(solution)/shard_map/grad_in/pallas_call | solution.py:508
  29.6 0.0 collective-permute-done.9
  29.6 1.6 %collective-permute-done.8 = bf16[288,128]{1,0:T(8,128)(2,1)S(1)} collective-permute-done((bf16[288,128]{1,0:T(8,128)(2,1)S(1)}, bf16[288,128]{1,0:T(8,128)(2,1)S(1)}, u32[]{:S(2)}, u32[]{:S(2)}) %collective-permute-start.8) | collective-permute-done | bytes 73760 | tf_op jit(solution)/shard_map/ppermute | solution.py:428
  31.2 1.4 %collective-permute-done.10 = bf16[288,128]{1,0:T(8,128)(2,1)S(1)} collective-permute-done((bf16[288,128]{1,0:T(8,128)(2,1)S(1)}, bf16[288,128]{1,0:T(8,128)(2,1)S(1)}, u32[]{:S(2)}, u32[]{:S(2)}) %collective-permute-start.10) | collective-permute-done | bytes 73760 | tf_op jit(solution)/shard_map/ppermute | solution.py:428
  32.6 0.1 collective-permute-start.11
  32.6 1.4 %collective-permute-done.11.other = f32[288,128]{1,0:T(8,128)S(1)} collective-permute-done((f32[288,128]{1,0:T(8,128)S(1)}, f32[288,128]{1,0:T(8,128)S(1)}, u32[]{:S(2)}, u32[]{:S(2)}) %collective-permute-start.11) | collective-permute-done | bytes 147488 | tf_op jit(solution)/shard_map/ppermute | solution.py:526
  34.0 0.9 %finish.1 = (f32[3,3,64,64]{3,2,1,0:T(8,128)}, f32[3,3,64,64]{3,2,1,0:T(8,128)}) custom-call(f32[288,128]{1,0:T(8,128)S(1)} %convert_add_fusion.mine, f32[288,128]{1,0:T(8,128)S(1)} %collective-permute-done.11.other), custom_call_target="tpu_custom_call" | custom-call | bytes 1048576 | tf_op jit(solution)/shard_map/finish/pallas_call | solution.py:528
  (3 shorter events, 0.1 us)
Async XLA Ops:
  2.4 5.0 %collective-permute-start = (bf16[128,128]{1,0:T(8,128)(2,1)S(1)}, bf16[128,128]{1,0:T(8,128)(2,1)S(1)}, u32[]{:S(2)}, u32[]{:S(2)}) collective-permute-start(bf16[128,128]{1,0:T(8,128)(2,1)S(1)} %get-tuple-element.33), channel_id=1, source_target_pairs={{0,1},{1,0},{2,3},{3,2},{8,9},{9,8},{10,11},{11,10},{16,17},{17,16... | collective-permute-start | bytes 98312 | tf_op jit(solution)/shard_map/ppermute | solution.py:51
  5.5 1.9 %collective-permute-start.1 = (bf16[128,128]{1,0:T(8,128)(2,1)S(1)}, bf16[128,128]{1,0:T(8,128)(2,1)S(1)}, u32[]{:S(2)}, u32[]{:S(2)}) collective-permute-start(bf16[128,128]{1,0:T(8,128)(2,1)S(1)} %get-tuple-element.34), channel_id=1, source_target_pairs={{0,8},{1,2},{2,1},{3,11},{8,0},{9,10},{10,9},{11,3},{16,24},{17,18... | collective-permute-start | bytes 98312 | tf_op jit(solution)/shard_map/ppermute | solution.py:51
  5.5 6.6 %collective-permute-start.2 = (bf16[2,128,256]{2,1,0:T(8,128)(2,1)S(1)}, bf16[2,128,256]{2,1,0:T(8,128)(2,1)S(1)}, u32[]{:S(2)}, u32[]{:S(2)}) collective-permute-start(bf16[2,128,256]{2,1,0:T(8,128)(2,1)S(1)} %get-tuple-element.41), channel_id=1, source_target_pairs={{0,4},{4,0},{8,12},{12,8},{16,20},{20,16},{24,28},{28,24},{1,5},{5... | collective-permute-start | bytes 393224 | tf_op jit(solution)/shard_map/ppermute | solution.py:51
  7.6 4.5 %collective-permute-start.3 = (bf16[128,128]{1,0:T(8,128)(2,1)S(1)}, bf16[128,128]{1,0:T(8,128)(2,1)S(1)}, u32[]{:S(2)}, u32[]{:S(2)}) collective-permute-start(bf16[128,128]{1,0:T(8,128)(2,1)S(1)} %corner.1), channel_id=1, source_target_pairs={{0,4},{4,0},{8,12},{12,8},{16,20},{20,16},{24,28},{28,24},{1,5},{5... | collective-permute-start | bytes 98312 | tf_op jit(solution)/shard_map/ppermute | solution.py:51
  13.2 1.4 %collective-permute-start.4 = (f32[288,128]{1,0:T(8,128)S(1)}, f32[288,128]{1,0:T(8,128)S(1)}, u32[]{:S(2)}, u32[]{:S(2)}) collective-permute-start(f32[288,128]{1,0:T(8,128)S(1)} %get-tuple-element.43), channel_id=1, source_target_pairs={{0,8},{8,0},{16,24},{24,16},{1,9},{9,1},{17,25},{25,17},{2,10},{10... | collective-permute-start | bytes 442376 | tf_op jit(solution)/shard_map/ppermute | solution.py:513
  14.7 5.7 %collective-permute-start.7 = (bf16[288,128]{1,0:T(8,128)(2,1)S(1)}, bf16[288,128]{1,0:T(8,128)(2,1)S(1)}, u32[]{:S(2)}, u32[]{:S(2)}) collective-permute-start(bf16[288,128]{1,0:T(8,128)(2,1)S(1)} %add_convert_fusion), channel_id=1, source_target_pairs={{0,20},{1,21},{2,22},{3,23},{4,16},{5,17},{6,18},{7,19},{8,28},{9,... | collective-permute-start | bytes 221192 | tf_op jit(solution)/shard_map/ppermute | solution.py:428
  17.2 4.4 %collective-permute-start.6 = (bf16[288,128]{1,0:T(8,128)(2,1)S(1)}, bf16[288,128]{1,0:T(8,128)(2,1)S(1)}, u32[]{:S(2)}, u32[]{:S(2)}) collective-permute-start(bf16[288,128]{1,0:T(8,128)(2,1)S(1)} %add_convert_fusion), channel_id=1, source_target_pairs={{0,4},{1,5},{2,6},{3,7},{4,0},{5,1},{6,2},{7,3},{8,12},{9,13},{10,... | collective-permute-start | bytes 221192 | tf_op jit(solution)/shard_map/ppermute | solution.py:428
  17.7 4.4 %collective-permute-start.5 = (bf16[288,128]{1,0:T(8,128)(2,1)S(1)}, bf16[288,128]{1,0:T(8,128)(2,1)S(1)}, u32[]{:S(2)}, u32[]{:S(2)}) collective-permute-start(bf16[288,128]{1,0:T(8,128)(2,1)S(1)} %add_convert_fusion), channel_id=1, source_target_pairs={{0,16},{1,17},{2,18},{3,19},{4,20},{5,21},{6,22},{7,23},{8,24},{9,... | collective-permute-start | bytes 221192 | tf_op jit(solution)/shard_map/ppermute | solution.py:428
  22.1 7.5 %collective-permute-start.9 = (bf16[288,128]{1,0:T(8,128)(2,1)S(1)}, bf16[288,128]{1,0:T(8,128)(2,1)S(1)}, u32[]{:S(2)}, u32[]{:S(2)}) collective-permute-start(bf16[288,128]{1,0:T(8,128)(2,1)S(1)} %convert_add_fusion.1), channel_id=1, source_target_pairs={{0,2},{1,3},{2,0},{3,1},{4,6},{5,7},{6,4},{7,5},{8,10},{9,11},{10,... | collective-permute-start | bytes 221192 | tf_op jit(solution)/shard_map/ppermute | solution.py:428
  26.3 4.9 %collective-permute-start.8 = (bf16[288,128]{1,0:T(8,128)(2,1)S(1)}, bf16[288,128]{1,0:T(8,128)(2,1)S(1)}, u32[]{:S(2)}, u32[]{:S(2)}) collective-permute-start(bf16[288,128]{1,0:T(8,128)(2,1)S(1)} %convert_add_fusion.1), channel_id=1, source_target_pairs={{0,1},{1,0},{2,3},{3,2},{4,5},{5,4},{6,7},{7,6},{8,9},{9,8},{10,11... | collective-permute-start | bytes 221192 | tf_op jit(solution)/shard_map/ppermute | solution.py:428
  26.3 6.3 %collective-permute-start.10 = (bf16[288,128]{1,0:T(8,128)(2,1)S(1)}, bf16[288,128]{1,0:T(8,128)(2,1)S(1)}, u32[]{:S(2)}, u32[]{:S(2)}) collective-permute-start(bf16[288,128]{1,0:T(8,128)(2,1)S(1)} %convert_add_fusion.1), channel_id=1, source_target_pairs={{0,3},{1,2},{2,1},{3,0},{4,7},{5,6},{6,5},{7,4},{8,11},{9,10},{10,... | collective-permute-start | bytes 221192 | tf_op jit(solution)/shard_map/ppermute | solution.py:428
  32.6 1.4 %collective-permute-start.11 = (f32[288,128]{1,0:T(8,128)S(1)}, f32[288,128]{1,0:T(8,128)S(1)}, u32[]{:S(2)}, u32[]{:S(2)}) collective-permute-start(f32[288,128]{1,0:T(8,128)S(1)} %convert_add_fusion.mine), channel_id=1, source_target_pairs={{0,8},{8,0},{16,24},{24,16},{1,9},{9,1},{17,25},{25,17},{2,10},{10... | collective-permute-start | bytes 442376 | tf_op jit(solution)/shard_map/ppermute | solution.py:526

commit v5 on v3

--- a/solution.py
+++ b/solution.py
@@ -280,7 +280,7 @@
 def outer_body(
     wf, x16, own, xi, xc, hids, g1_in, g2_in,
     strip_a, strip_b, row_a, row_b, corner_a, corner_b,
-    acts_o, hids_o, mine, other, xo, grads,
+    acts_o, hids_o, mine, other, xo,
 ):
     rows, ch2, cols = x16.shape
     ch = ch2 // 2
@@ -352,13 +352,14 @@
             rhs = xi[r] if 0 <= r < rows else xo[0, 1 if r < 0 else 2]
             lhs = [row if h == r - 1 + k else zero_row for k in range(3)]
             g1 = add_grads(g1, lhs, rhs)
-    grads[0 : 3 * ch, :] = g1[:, : 2 * ch]
-    grads[3 * ch : 6 * ch, :] = g2[:, : 2 * ch]
-    grads[6 * ch : 9 * ch, :] = jnp.concatenate([g1[:, 2 * ch :], g2[:, 2 * ch :]], 1)
     count = mine.shape[0]
-    core = lax.axis_index("dp") % 2
-    mine[...] = grads[pl.ds(core * count, count), :]
-    other[...] = grads[pl.ds((1 - core) * count, count), :]
+    cut = count - 3 * ch
+    low = jnp.concatenate([g1[:, : 2 * ch], g2[:cut, : 2 * ch]], 0)
+    tail = jnp.concatenate([g1[:, 2 * ch :], g2[:, 2 * ch :]], 1)
+    high = jnp.concatenate([g2[cut:, : 2 * ch], tail], 0)
+    leads = lax.axis_index("dp") % 2 == 0
+    mine[...] = jnp.where(leads, low, high)
+    other[...] = jnp.where(leads, high, low)
 
 
 def back_body(flip, kernel, mid, ends, out, weights, wide):
@@ -487,7 +488,7 @@
     acts_o, hids_o, mine, other = kernel_call(
         optional(outer_body, [True] * 8 + [True, two_cols] + [True, two_rows] * 2),
         [shifted(4), shifted(4), half, half],
-        [pltpu.VMEM((2, 4, 3 * ch, cols), BF), pltpu.VMEM((9 * ch, LANES), F32)],
+        [pltpu.VMEM((2, 4, 3 * ch, cols), BF)],
         flops=1 << 28,
         name="outer",
     )(wf, x16, own, xi, xc, hids, g1, g2, *strips, *got_rows, *corners)

time: 35.1 us -> 35.1 us (level)
  no operation moved by 1% of the time
where the time goes in v5:
time: 35.1 us; the launch traced here: 34.9 us
  starting transfers between devices  16 us (46%)
  Pallas kernels  9.5 us (27%)
  waiting for transfers between devices  8.69 us (25%)
  between operations  0.69 us (2%)
    ppermute x6, starting transfers between devices, exchange(): total = total + lax.ppermute(sent, axes, perm).astype(F32)  9.2 us
    ppermute x4, starting transfers between devices, swap(): return lax.ppermute(array, ('dp', axis), perm)  6.61 us
    ppermute x6, waiting for transfers between devices, exchange(): total = total + lax.ppermute(sent, axes, perm).astype(F32)  5.4 us
    pallas_call x2, Pallas kernels, back(): kernel_call(functools.partial(back_body, flip), [sds(images.shape, BF)],...  3.17 us
    pallas_call x1, Pallas kernels, on_device(): kernel_call(optional(inner_body, [True] * 5 + [two_cols]), [shifted(rows)...  2.37 us
    pallas_call x1, Pallas kernels, on_device(): pack(*[pltpu.with_memory_space_constraint(v, pltpu.HBM) for v in (images,...  1.76 us
    ppermute x1, waiting for transfers between devices, on_device(): total_half = mine + lax.ppermute(other, 'dp', partner)  1.36 us
    ppermute x1, waiting for transfers between devices, on_device(): rest = lax.ppermute(total_half, 'dp', partner)  1.36 us
  transfers between devices with their start and end apart: 12, of which 9 were waited for; matrix products, arithmetic and copies ran while one was open for 0% of the time, Pallas kernels for 16%

profile of v5, /device:TPU:0, one launch (start us, length us, event | category | flops | bytes accessed | tf_op | source)
XLA Modules:
  0.0 34.9 jit_solution(3741622269139632778)
XLA Ops:
  0.6 1.8 %pack.1 = (bf16[16,128,256]{2,1,0:T(8,128)(2,1)S(1)}, bf16[2,128,128]{2,1,0:T(8,128)(2,1)S(1)}, bf16[3,3,64,64]{3,2,1,0:T(8,128)(2,1)S(1)}, bf16[3,3,64,64]{3,2,...) custom-call(bf16[1,64,16,256]{3,2,1,0:T(8,128)(2,1)} %refs_0_.1, ...), custom_call_target="tpu_custom_call" | custom-call | flops 134217728 | bytes 1048576 | tf_op jit(solution)/shard_map/pack/pallas_call | solution.py:465
  2.4 3.1 %collective-permute-start = (bf16[128,128]{1,0:T(8,128)(2,1)S(1)}, bf16[128,128]{1,0:T(8,128)(2,1)S(1)}, u32[]{:S(2)}, u32[]{:S(2)}) collective-permute-start(bf16[128,128]{1,0:T(8,128)(2,1)S(1)} %get-tuple-element.32), channel_id=1, source_target_pairs={{0,1},{1,0},{2,3},{3,2},{8,9},{9,8},{10,11},{11,10},{16,17},{17,16... | collective-permute-start | bytes 98312 | tf_op jit(solution)/shard_map/ppermute | solution.py:51
  5.5 0.0 collective-permute-start.1
  5.5 1.5 %collective-permute-start.2 = (bf16[2,128,256]{2,1,0:T(8,128)(2,1)S(1)}, bf16[2,128,256]{2,1,0:T(8,128)(2,1)S(1)}, u32[]{:S(2)}, u32[]{:S(2)}) collective-permute-start(bf16[2,128,256]{2,1,0:T(8,128)(2,1)S(1)} %get-tuple-element.40), channel_id=1, source_target_pairs={{0,4},{4,0},{8,12},{12,8},{16,20},{20,16},{24,28},{28,24},{1,5},{5... | collective-permute-start | bytes 393224 | tf_op jit(solution)/shard_map/ppermute | solution.py:51
  7.0 0.4 %collective-permute-done.refs_4_.refs_0_.refs_8_ = bf16[128,128]{1,0:T(8,128)(2,1)S(1)} collective-permute-done((bf16[128,128]{1,0:T(8,128)(2,1)S(1)}, bf16[128,128]{1,0:T(8,128)(2,1)S(1)}, u32[]{:S(2)}, u32[]{:S(2)}) %collective-permute-start) | collective-permute-done | bytes 32800 | tf_op jit(solution)/shard_map/ppermute | solution.py:51
  7.4 0.0 collective-permute-done.1.refs_5_.refs_1_.refs_9_
  7.4 0.2 corner.1
  7.6 2.0 %collective-permute-start.3 = (bf16[128,128]{1,0:T(8,128)(2,1)S(1)}, bf16[128,128]{1,0:T(8,128)(2,1)S(1)}, u32[]{:S(2)}, u32[]{:S(2)}) collective-permute-start(bf16[128,128]{1,0:T(8,128)(2,1)S(1)} %corner.1), channel_id=1, source_target_pairs={{0,4},{4,0},{8,12},{12,8},{16,20},{20,16},{24,28},{28,24},{1,5},{5... | collective-permute-start | bytes 98312 | tf_op jit(solution)/shard_map/ppermute | solution.py:51
  9.6 2.4 %inner.1 = (bf16[16,192,256]{2,1,0:T(8,128)(2,1)S(1)}, bf16[16,192,256]{2,1,0:T(8,128)(2,1)S(1)}, bf16[14,192,256]{2,1,0:T(8,128)(2,1)S(1)}, bf16[14,192,256]{2,...) custom-call(bf16[3,3,64,64]{3,2,1,0:T(8,128)(2,1)S(1)} %get-tuple-element.28, ...), custom_call_target="tpu_custom_call" | custom-call | flops 1073741824 | bytes 1048576 | tf_op jit(solution)/shard_map/inner/pallas_call | solution.py:480
  12.0 0.2 collective-permute-done.3.refs_11_
  12.1 0.0 collective-permute-done.2.refs_10_
  12.1 1.1 %outer.1 = (bf16[4,192,256]{2,1,0:T(8,128)(2,1)S(1)}, bf16[4,192,256]{2,1,0:T(8,128)(2,1)S(1)}, f32[288,128]{1,0:T(8,128)S(1)}, f32[288,128]{1,0:T(8,128)S(1)}) custom-call(bf16[2,128,768]{2,1,0:T(8,128)(2,1)S(1)} %get-tuple-element.34.refs_0_, bf16[16,128,256]{2,1,0:T(8,128)(2,1)S(1)} %get-tuple-element.30.refs_2_.refs_1_, ...), custom_call_target="tpu_custom_call" | custom-call | flops 268435456 | bytes 1048576 | tf_op jit(solution)/shard_map/outer/pallas_call | solution.py:488
  13.2 0.1 collective-permute-start.4
  13.3 1.4 %collective-permute-done.4 = f32[288,128]{1,0:T(8,128)S(1)} collective-permute-done((f32[288,128]{1,0:T(8,128)S(1)}, f32[288,128]{1,0:T(8,128)S(1)}, u32[]{:S(2)}, u32[]{:S(2)}) %collective-permute-start.4) | collective-permute-done | bytes 147488 | tf_op jit(solution)/shard_map/ppermute | solution.py:509
  14.7 2.5 %collective-permute-start.7 = (bf16[288,128]{1,0:T(8,128)(2,1)S(1)}, bf16[288,128]{1,0:T(8,128)(2,1)S(1)}, u32[]{:S(2)}, u32[]{:S(2)}) collective-permute-start(bf16[288,128]{1,0:T(8,128)(2,1)S(1)} %add_convert_fusion), channel_id=1, source_target_pairs={{0,20},{1,21},{2,22},{3,23},{4,16},{5,17},{6,18},{7,19},{8,28},{9,... | collective-permute-start | bytes 221192 | tf_op jit(solution)/shard_map/ppermute | solution.py:423
  17.2 0.5 %collective-permute-start.6 = (bf16[288,128]{1,0:T(8,128)(2,1)S(1)}, bf16[288,128]{1,0:T(8,128)(2,1)S(1)}, u32[]{:S(2)}, u32[]{:S(2)}) collective-permute-start(bf16[288,128]{1,0:T(8,128)(2,1)S(1)} %add_convert_fusion), channel_id=1, source_target_pairs={{0,4},{1,5},{2,6},{3,7},{4,0},{5,1},{6,2},{7,3},{8,12},{9,13},{10,... | collective-permute-start | bytes 221192 | tf_op jit(solution)/shard_map/ppermute | solution.py:423
  17.7 0.5 %collective-permute-start.5 = (bf16[288,128]{1,0:T(8,128)(2,1)S(1)}, bf16[288,128]{1,0:T(8,128)(2,1)S(1)}, u32[]{:S(2)}, u32[]{:S(2)}) collective-permute-start(bf16[288,128]{1,0:T(8,128)(2,1)S(1)} %add_convert_fusion), channel_id=1, source_target_pairs={{0,16},{1,17},{2,18},{3,19},{4,20},{5,21},{6,22},{7,23},{8,24},{9,... | collective-permute-start | bytes 221192 | tf_op jit(solution)/shard_map/ppermute | solution.py:423
  18.2 1.5 %out.1 = bf16[1,64,16,256]{3,2,1,0:T(8,128)(2,1)} custom-call(bf16[3,3,64,64]{3,2,1,0:T(8,128)(2,1)S(1)} %get-tuple-element.29.refs_1_.kernel, bf16[14,192,256]{2,1,0:T(8,128)(2,1)S(1)} %get-tuple-element.43.mid, bf16[4,192,256]{2,1,0:T(8,128)(2,1)S(1)} %get-tuple-element.44.ends), custom_call_target="tpu_custom_call" | custom-call | flops 536870912 | bytes 1048576 | tf_op jit(solution)/shard_map/out/pallas_call | solution.py:497
  19.8 0.6 %collective-permute-done.7 = bf16[288,128]{1,0:T(8,128)(2,1)S(1)} collective-permute-done((bf16[288,128]{1,0:T(8,128)(2,1)S(1)}, bf16[288,128]{1,0:T(8,128)(2,1)S(1)}, u32[]{:S(2)}, u32[]{:S(2)}) %collective-permute-start.7) | collective-permute-done | bytes 73760 | tf_op jit(solution)/shard_map/ppermute | solution.py:423
  20.4 1.2 %collective-permute-done.6 = bf16[288,128]{1,0:T(8,128)(2,1)S(1)} collective-permute-done((bf16[288,128]{1,0:T(8,128)(2,1)S(1)}, bf16[288,128]{1,0:T(8,128)(2,1)S(1)}, u32[]{:S(2)}, u32[]{:S(2)}) %collective-permute-start.6) | collective-permute-done | bytes 73760 | tf_op jit(solution)/shard_map/ppermute | solution.py:423
  21.6 0.4 %collective-permute-done.5 = bf16[288,128]{1,0:T(8,128)(2,1)S(1)} collective-permute-done((bf16[288,128]{1,0:T(8,128)(2,1)S(1)}, bf16[288,128]{1,0:T(8,128)(2,1)S(1)}, u32[]{:S(2)}, u32[]{:S(2)}) %collective-permute-start.5) | collective-permute-done | bytes 73760 | tf_op jit(solution)/shard_map/ppermute | solution.py:423
  22.1 4.1 %collective-permute-start.9 = (bf16[288,128]{1,0:T(8,128)(2,1)S(1)}, bf16[288,128]{1,0:T(8,128)(2,1)S(1)}, u32[]{:S(2)}, u32[]{:S(2)}) collective-permute-start(bf16[288,128]{1,0:T(8,128)(2,1)S(1)} %convert_add_fusion.1), channel_id=1, source_target_pairs={{0,2},{1,3},{2,0},{3,1},{4,6},{5,7},{6,4},{7,5},{8,10},{9,11},{10,... | collective-permute-start | bytes 221192 | tf_op jit(solution)/shard_map/ppermute | solution.py:423
  26.2 0.0 collective-permute-start.8
  26.3 1.5 %collective-permute-start.10 = (bf16[288,128]{1,0:T(8,128)(2,1)S(1)}, bf16[288,128]{1,0:T(8,128)(2,1)S(1)}, u32[]{:S(2)}, u32[]{:S(2)}) collective-permute-start(bf16[288,128]{1,0:T(8,128)(2,1)S(1)} %convert_add_fusion.1), channel_id=1, source_target_pairs={{0,3},{1,2},{2,1},{3,0},{4,7},{5,6},{6,5},{7,4},{8,11},{9,10},{10,... | collective-permute-start | bytes 221192 | tf_op jit(solution)/shard_map/ppermute | solution.py:423
  27.8 1.6 %grad_in.1 = bf16[1,64,16,256]{3,2,1,0:T(8,128)(2,1)} custom-call(bf16[3,3,64,64]{3,2,1,0:T(8,128)(2,1)S(1)} %get-tuple-element.28.refs_0_.kernel, bf16[14,192,256]{2,1,0:T(8,128)(2,1)S(1)} %get-tuple-element.37.refs_5_.mid, bf16[4,192,256]{2,1,0:T(8,128)(2,1)S(1)} %get-tuple-element.47.ends), custom_call_target="tpu_custom_call" | custom-call | flops 536870912 | bytes 1048576 | tf_op jit(solution)/shard_map/grad_in/pallas_call | solution.py:497
  29.4 0.0 collective-permute-done.9
  29.4 1.7 %collective-permute-done.8 = bf16[288,128]{1,0:T(8,128)(2,1)S(1)} collective-permute-done((bf16[288,128]{1,0:T(8,128)(2,1)S(1)}, bf16[288,128]{1,0:T(8,128)(2,1)S(1)}, u32[]{:S(2)}, u32[]{:S(2)}) %collective-permute-start.8) | collective-permute-done | bytes 73760 | tf_op jit(solution)/shard_map/ppermute | solution.py:423
  31.2 1.4 %collective-permute-done.10 = bf16[288,128]{1,0:T(8,128)(2,1)S(1)} collective-permute-done((bf16[288,128]{1,0:T(8,128)(2,1)S(1)}, bf16[288,128]{1,0:T(8,128)(2,1)S(1)}, u32[]{:S(2)}, u32[]{:S(2)}) %collective-permute-start.10) | collective-permute-done | bytes 73760 | tf_op jit(solution)/shard_map/ppermute | solution.py:423
  32.6 0.1 collective-permute-start.11
  32.6 1.4 %collective-permute-done.11.other = f32[288,128]{1,0:T(8,128)S(1)} collective-permute-done((f32[288,128]{1,0:T(8,128)S(1)}, f32[288,128]{1,0:T(8,128)S(1)}, u32[]{:S(2)}, u32[]{:S(2)}) %collective-permute-start.11) | collective-permute-done | bytes 147488 | tf_op jit(solution)/shard_map/ppermute | solution.py:522
  34.0 0.9 %finish.1 = (f32[3,3,64,64]{3,2,1,0:T(8,128)}, f32[3,3,64,64]{3,2,1,0:T(8,128)}) custom-call(f32[288,128]{1,0:T(8,128)S(1)} %convert_add_fusion.mine, f32[288,128]{1,0:T(8,128)S(1)} %collective-permute-done.11.other), custom_call_target="tpu_custom_call" | custom-call | bytes 1048576 | tf_op jit(solution)/shard_map/finish/pallas_call | solution.py:524
  (3 shorter events, 0.1 us)
Async XLA Ops:
  2.4 5.0 %collective-permute-start = (bf16[128,128]{1,0:T(8,128)(2,1)S(1)}, bf16[128,128]{1,0:T(8,128)(2,1)S(1)}, u32[]{:S(2)}, u32[]{:S(2)}) collective-permute-start(bf16[128,128]{1,0:T(8,128)(2,1)S(1)} %get-tuple-element.32), channel_id=1, source_target_pairs={{0,1},{1,0},{2,3},{3,2},{8,9},{9,8},{10,11},{11,10},{16,17},{17,16... | collective-permute-start | bytes 98312 | tf_op jit(solution)/shard_map/ppermute | solution.py:51
  5.5 1.9 %collective-permute-start.1 = (bf16[128,128]{1,0:T(8,128)(2,1)S(1)}, bf16[128,128]{1,0:T(8,128)(2,1)S(1)}, u32[]{:S(2)}, u32[]{:S(2)}) collective-permute-start(bf16[128,128]{1,0:T(8,128)(2,1)S(1)} %get-tuple-element.33), channel_id=1, source_target_pairs={{0,8},{1,2},{2,1},{3,11},{8,0},{9,10},{10,9},{11,3},{16,24},{17,18... | collective-permute-start | bytes 98312 | tf_op jit(solution)/shard_map/ppermute | solution.py:51
  5.5 6.6 %collective-permute-start.2 = (bf16[2,128,256]{2,1,0:T(8,128)(2,1)S(1)}, bf16[2,128,256]{2,1,0:T(8,128)(2,1)S(1)}, u32[]{:S(2)}, u32[]{:S(2)}) collective-permute-start(bf16[2,128,256]{2,1,0:T(8,128)(2,1)S(1)} %get-tuple-element.40), channel_id=1, source_target_pairs={{0,4},{4,0},{8,12},{12,8},{16,20},{20,16},{24,28},{28,24},{1,5},{5... | collective-permute-start | bytes 393224 | tf_op jit(solution)/shard_map/ppermute | solution.py:51
  7.6 4.5 %collective-permute-start.3 = (bf16[128,128]{1,0:T(8,128)(2,1)S(1)}, bf16[128,128]{1,0:T(8,128)(2,1)S(1)}, u32[]{:S(2)}, u32[]{:S(2)}) collective-permute-start(bf16[128,128]{1,0:T(8,128)(2,1)S(1)} %corner.1), channel_id=1, source_target_pairs={{0,4},{4,0},{8,12},{12,8},{16,20},{20,16},{24,28},{28,24},{1,5},{5... | collective-permute-start | bytes 98312 | tf_op jit(solution)/shard_map/ppermute | solution.py:51
  13.2 1.4 %collective-permute-start.4 = (f32[288,128]{1,0:T(8,128)S(1)}, f32[288,128]{1,0:T(8,128)S(1)}, u32[]{:S(2)}, u32[]{:S(2)}) collective-permute-start(f32[288,128]{1,0:T(8,128)S(1)} %get-tuple-element.42), channel_id=1, source_target_pairs={{0,8},{8,0},{16,24},{24,16},{1,9},{9,1},{17,25},{25,17},{2,10},{10... | collective-permute-start | bytes 442376 | tf_op jit(solution)/shard_map/ppermute | solution.py:509
  14.7 5.7 %collective-permute-start.7 = (bf16[288,128]{1,0:T(8,128)(2,1)S(1)}, bf16[288,128]{1,0:T(8,128)(2,1)S(1)}, u32[]{:S(2)}, u32[]{:S(2)}) collective-permute-start(bf16[288,128]{1,0:T(8,128)(2,1)S(1)} %add_convert_fusion), channel_id=1, source_target_pairs={{0,20},{1,21},{2,22},{3,23},{4,16},{5,17},{6,18},{7,19},{8,28},{9,... | collective-permute-start | bytes 221192 | tf_op jit(solution)/shard_map/ppermute | solution.py:423
  17.2 4.4 %collective-permute-start.6 = (bf16[288,128]{1,0:T(8,128)(2,1)S(1)}, bf16[288,128]{1,0:T(8,128)(2,1)S(1)}, u32[]{:S(2)}, u32[]{:S(2)}) collective-permute-start(bf16[288,128]{1,0:T(8,128)(2,1)S(1)} %add_convert_fusion), channel_id=1, source_target_pairs={{0,4},{1,5},{2,6},{3,7},{4,0},{5,1},{6,2},{7,3},{8,12},{9,13},{10,... | collective-permute-start | bytes 221192 | tf_op jit(solution)/shard_map/ppermute | solution.py:423
  17.7 4.4 %collective-permute-start.5 = (bf16[288,128]{1,0:T(8,128)(2,1)S(1)}, bf16[288,128]{1,0:T(8,128)(2,1)S(1)}, u32[]{:S(2)}, u32[]{:S(2)}) collective-permute-start(bf16[288,128]{1,0:T(8,128)(2,1)S(1)} %add_convert_fusion), channel_id=1, source_target_pairs={{0,16},{1,17},{2,18},{3,19},{4,20},{5,21},{6,22},{7,23},{8,24},{9,... | collective-permute-start | bytes 221192 | tf_op jit(solution)/shard_map/ppermute | solution.py:423
  22.1 7.3 %collective-permute-start.9 = (bf16[288,128]{1,0:T(8,128)(2,1)S(1)}, bf16[288,128]{1,0:T(8,128)(2,1)S(1)}, u32[]{:S(2)}, u32[]{:S(2)}) collective-permute-start(bf16[288,128]{1,0:T(8,128)(2,1)S(1)} %convert_add_fusion.1), channel_id=1, source_target_pairs={{0,2},{1,3},{2,0},{3,1},{4,6},{5,7},{6,4},{7,5},{8,10},{9,11},{10,... | collective-permute-start | bytes 221192 | tf_op jit(solution)/shard_map/ppermute | solution.py:423
  26.2 4.9 %collective-permute-start.8 = (bf16[288,128]{1,0:T(8,128)(2,1)S(1)}, bf16[288,128]{1,0:T(8,128)(2,1)S(1)}, u32[]{:S(2)}, u32[]{:S(2)}) collective-permute-start(bf16[288,128]{1,0:T(8,128)(2,1)S(1)} %convert_add_fusion.1), channel_id=1, source_target_pairs={{0,1},{1,0},{2,3},{3,2},{4,5},{5,4},{6,7},{7,6},{8,9},{9,8},{10,11... | collective-permute-start | bytes 221192 | tf_op jit(solution)/shard_map/ppermute | solution.py:423
  26.3 6.3 %collective-permute-start.10 = (bf16[288,128]{1,0:T(8,128)(2,1)S(1)}, bf16[288,128]{1,0:T(8,128)(2,1)S(1)}, u32[]{:S(2)}, u32[]{:S(2)}) collective-permute-start(bf16[288,128]{1,0:T(8,128)(2,1)S(1)} %convert_add_fusion.1), channel_id=1, source_target_pairs={{0,3},{1,2},{2,1},{3,0},{4,7},{5,6},{6,5},{7,4},{8,11},{9,10},{10,... | collective-permute-start | bytes 221192 | tf_op jit(solution)/shard_map/ppermute | solution.py:423
  32.6 1.4 %collective-permute-start.11 = (f32[288,128]{1,0:T(8,128)S(1)}, f32[288,128]{1,0:T(8,128)S(1)}, u32[]{:S(2)}, u32[]{:S(2)}) collective-permute-start(f32[288,128]{1,0:T(8,128)S(1)} %convert_add_fusion.mine), channel_id=1, source_target_pairs={{0,8},{8,0},{16,24},{24,16},{1,9},{9,1},{17,25},{25,17},{2,10},{10... | collective-permute-start | bytes 442376 | tf_op jit(solution)/shard_map/ppermute | solution.py:522
